TPU v7x, 32 devices: a 4x2x2 block of a 4x4x8 slice. The times are simulated.
32 devices in a mesh: dp: 4 (over y, z), cp: 8 (over x, core).
Axes of the slice: x: 4, y: 2, z: 2, core: 2. Of those that a mesh axis runs over, the one named last changes fastest.
The devices are a block of a 4x4x8 slice.
Arguments:
- x_act: bfloat16 [12288, 2048], P(('dp', 'cp')), parts along dimension 0
- seg_ids: int32 [12288], P(('dp', 'cp')), parts along dimension 0
- w_q: bfloat16 [2048, 32, 64], replicated
- w_k: bfloat16 [2048, 8, 64], replicated
- w_v: bfloat16 [2048, 8, 64], replicated
- w_o: bfloat16 [2048, 32, 64], replicated
- dy_act: bfloat16 [12288, 2048], P(('dp', 'cp')), parts along dimension 0
Outputs:
- output 1: bfloat16 [12288, 2048], P(('dp', 'cp')), parts along dimension 0
- output 2: bfloat16 [12288, 2048], P(('dp', 'cp')), parts along dimension 0
- output 3: float32 [8192, 32, 64], P(('dp', 'cp')), parts along dimension 0
- output 4: float32 [8192, 8, 64], P(('dp', 'cp')), parts along dimension 0
- output 5: float32 [8192, 8, 64], P(('dp', 'cp')), parts along dimension 0
- output 6: float32 [8192, 32, 64], P(('dp', 'cp')), parts along dimension 0
There are 4 independent parts. A program takes and returns all parts, laid end to end along the dimension named above; an argument that names none is the same for every part.
All inputs are finite; a program needn't handle non-finite values.
Results may differ from a plain program's by a relative error of at most 0.02.
Values are sent between devices in bfloat16 or wider.
A program may use at most 768 MiB of HBM per device.

v0:
```python
import jax
import jax.numpy as jnp
from jax import lax
from jax.sharding import PartitionSpec as P


def block_mask(seg_q, seg_k, q_first, k_first):
    query_pos = q_first + jnp.arange(seg_q.shape[0])
    key_pos = k_first + jnp.arange(seg_k.shape[0])
    return (seg_q[:, None] == seg_k[None, :]) & (key_pos[None, :] <= query_pos[:, None])


def block_active(seg_q, seg_k, my_index, src_index):
    return (src_index == my_index) | ((src_index < my_index) & (seg_k[-1] == seg_q[0]))


def attend_block(run_stats, q_loc, k_blk, v_blk, allowed, score_scale):
    row_max, row_sum, out_acc = run_stats
    scores = jnp.einsum('qkgd,skd->kqgs', q_loc, k_blk, preferred_element_type=jnp.float32) * score_scale
    scores = jnp.where(allowed[None, :, None, :], scores, -jnp.inf)
    new_max = jnp.maximum(row_max, jnp.max(scores, axis=-1))
    weights = jnp.exp(scores - new_max[..., None])
    factor = jnp.exp(row_max - new_max)
    new_sum = row_sum * factor + jnp.sum(weights, axis=-1)
    new_out = out_acc * factor[..., None] + jnp.einsum('kqgs,skd->kqgd', weights.astype(jnp.bfloat16), v_blk, preferred_element_type=jnp.float32)
    return new_max, new_sum, new_out


def grad_block(q_loc, do_loc, log_norm, row_delta, k_blk, v_blk, allowed, score_scale):
    scores = jnp.einsum('qkgd,skd->kqgs', q_loc, k_blk, preferred_element_type=jnp.float32) * score_scale
    attn_prob = jnp.exp(jnp.where(allowed[None, :, None, :], scores, -jnp.inf) - log_norm[..., None])
    dprobs = jnp.einsum('qkgd,skd->kqgs', do_loc, v_blk, preferred_element_type=jnp.float32)
    dscores = (attn_prob * (dprobs - row_delta[..., None])).astype(jnp.bfloat16)
    dq_part = jnp.einsum('kqgs,skd->kqgd', dscores, k_blk, preferred_element_type=jnp.float32)
    dk_part = jnp.einsum('kqgs,qkgd->ksd', dscores, q_loc, preferred_element_type=jnp.float32)
    dv_part = jnp.einsum('kqgs,qkgd->ksd', attn_prob.astype(jnp.bfloat16), do_loc, preferred_element_type=jnp.float32)
    return dq_part, dk_part, dv_part


def solution(mesh):
    group_count = mesh.shape['cp']
    shift_pairs = [(source, (source + 1) % group_count) for source in range(group_count)]
    row_spec = P(('dp', 'cp'), None)
    tok_spec = P(('dp', 'cp'))
    weight_spec = P(None, None, None)
    grad_spec = P(('dp', 'cp'), None, None)

    def local_step(x_act, seg_ids, w_q, w_k, w_v, w_o, dy_act):
        tok_count = x_act.shape[0]
        model_dim, q_heads, head_dim = w_q.shape
        kv_heads = w_k.shape[1]
        group_size = q_heads // kv_heads
        score_scale = head_dim ** -0.5
        my_index = lax.axis_index('cp')
        q_first = my_index * tok_count
        w_q4 = w_q.reshape(model_dim, kv_heads, group_size, head_dim)
        w_o4 = w_o.reshape(model_dim, kv_heads, group_size, head_dim)
        q_loc = jnp.einsum('sm,mkgd->skgd', x_act, w_q4, preferred_element_type=jnp.float32).astype(jnp.bfloat16)
        k_loc = jnp.einsum('sm,mkd->skd', x_act, w_k, preferred_element_type=jnp.float32).astype(jnp.bfloat16)
        v_loc = jnp.einsum('sm,mkd->skd', x_act, w_v, preferred_element_type=jnp.float32).astype(jnp.bfloat16)

        def forward_step(run_stats, k_blk, v_blk, seg_blk, step_num):
            src_index = (my_index - step_num) % group_count

            def active_branch(stats_in):
                allowed = block_mask(seg_ids, seg_blk, q_first, src_index * tok_count)
                return attend_block(stats_in, q_loc, k_blk, v_blk, allowed, score_scale)

            return lax.cond(block_active(seg_ids, seg_blk, my_index, src_index),
                            active_branch, lambda stats_in: stats_in, run_stats)

        def forward_body(step_num, carry_in):
            run_stats, k_blk, v_blk, seg_blk = carry_in
            run_stats = forward_step(run_stats, k_blk, v_blk, seg_blk, step_num)
            k_blk, v_blk, seg_blk = lax.ppermute((k_blk, v_blk, seg_blk), 'cp', shift_pairs)
            return run_stats, k_blk, v_blk, seg_blk

        stat_shape = (kv_heads, tok_count, group_size)
        start_stats = (jnp.full(stat_shape, -1e30, jnp.float32), jnp.zeros(stat_shape, jnp.float32),
                       jnp.zeros(stat_shape + (head_dim,), jnp.float32))
        run_stats, k_blk, v_blk, seg_blk = lax.fori_loop(0, group_count - 1, forward_body, (start_stats, k_loc, v_loc, seg_ids))
        row_max, row_sum, out_acc = forward_step(run_stats, k_blk, v_blk, seg_blk, group_count - 1)
        o_loc = (out_acc / row_sum[..., None]).astype(jnp.bfloat16)
        log_norm = row_max + jnp.log(row_sum)
        y_out = jnp.einsum('kqgd,mkgd->qm', o_loc, w_o4, preferred_element_type=jnp.float32).astype(jnp.bfloat16)

        do_loc = jnp.einsum('qm,mkgd->qkgd', dy_act, w_o4, preferred_element_type=jnp.float32).astype(jnp.bfloat16)
        row_delta = jnp.einsum('qkgd,kqgd->kqg', do_loc, o_loc, preferred_element_type=jnp.float32)
        dwo_part = jnp.einsum('qm,kqgd->mkgd', dy_act, o_loc, preferred_element_type=jnp.float32).reshape(model_dim, q_heads, head_dim)

        def backward_step(grads_in, k_blk, v_blk, seg_blk, step_num):
            src_index = (my_index - step_num) % group_count

            def active_branch(accs_in):
                dq_acc, dk_acc, dv_acc = accs_in
                allowed = block_mask(seg_ids, seg_blk, q_first, src_index * tok_count)
                dq_part, dk_part, dv_part = grad_block(q_loc, do_loc, log_norm, row_delta, k_blk, v_blk, allowed, score_scale)
                return dq_acc + dq_part, dk_acc + dk_part, dv_acc + dv_part

            return lax.cond(block_active(seg_ids, seg_blk, my_index, src_index),
                            active_branch, lambda accs_in: accs_in, grads_in)

        def backward_body(step_num, carry_in):
            dq_acc, dk_acc, dv_acc, k_blk, v_blk, seg_blk = carry_in
            dq_acc, dk_acc, dv_acc = backward_step((dq_acc, dk_acc, dv_acc), k_blk, v_blk, seg_blk, step_num)
            k_blk, v_blk, seg_blk, dk_acc, dv_acc = lax.ppermute((k_blk, v_blk, seg_blk, dk_acc, dv_acc), 'cp', shift_pairs)
            return dq_acc, dk_acc, dv_acc, k_blk, v_blk, seg_blk

        kv_zeros = jnp.zeros((kv_heads, tok_count, head_dim), jnp.float32)
        dq_zeros = jnp.zeros((kv_heads, tok_count, group_size, head_dim), jnp.float32)
        dq_acc, dk_acc, dv_acc, k_blk, v_blk, seg_blk = lax.fori_loop(
            0, group_count - 1, backward_body, (dq_zeros, kv_zeros, kv_zeros, k_loc, v_loc, seg_ids))
        dq_acc, dk_acc, dv_acc = backward_step((dq_acc, dk_acc, dv_acc), k_blk, v_blk, seg_blk, group_count - 1)
        dk_acc, dv_acc = lax.ppermute((dk_acc, dv_acc), 'cp', shift_pairs)

        grad_q = (dq_acc * score_scale).astype(jnp.bfloat16)
        grad_k = (dk_acc * score_scale).astype(jnp.bfloat16)
        grad_v = dv_acc.astype(jnp.bfloat16)
        dx_wide = (jnp.einsum('kqgd,mkgd->qm', grad_q, w_q4, preferred_element_type=jnp.float32)
                   + jnp.einsum('ksd,mkd->sm', grad_k, w_k, preferred_element_type=jnp.float32)
                   + jnp.einsum('ksd,mkd->sm', grad_v, w_v, preferred_element_type=jnp.float32))
        dx_out = dx_wide.astype(jnp.bfloat16)
        dwq_part = jnp.einsum('qm,kqgd->mkgd', x_act, grad_q, preferred_element_type=jnp.float32).reshape(model_dim, q_heads, head_dim)
        dwk_part = jnp.einsum('sm,ksd->mkd', x_act, grad_k, preferred_element_type=jnp.float32)
        dwv_part = jnp.einsum('sm,ksd->mkd', x_act, grad_v, preferred_element_type=jnp.float32)

        def reduce_rows(part_sum):
            return lax.psum_scatter(part_sum, 'cp', scatter_dimension=0, tiled=True)

        return (y_out, dx_out, reduce_rows(dwq_part), reduce_rows(dwk_part),
                reduce_rows(dwv_part), reduce_rows(dwo_part))

    return jax.shard_map(local_step, mesh=mesh,
                         in_specs=(row_spec, tok_spec, weight_spec, weight_spec, weight_spec, weight_spec, row_spec),
                         out_specs=(row_spec, row_spec, grad_spec, grad_spec, grad_spec, grad_spec),
                         check_vma=False)
```

profile of v0, /device:TPU:81, one launch (start us, length us, event | category | flops | bytes accessed | tf_op | source)
XLA Modules:
  0.0 967.7 jit_solution(3483076782760418288)
XLA Ops:
  10.6 3.4 fusion.83
  19.4 4.5 fusion.84
  27.5 204.4 %while.50 = (s32[]{:T(128)}, f32[8,384,4]{1,2,0:T(4,128)S(1)}, f32[8,384,4]{1,2,0:T(4,128)S(1)}, f32[8,384,4,64]{1,3,2,0:T(8,128)}, bf16[384,8,64]{0,2,1:T(8,128...) while((s32[]{:T(128)}, f32[8,384,4]{1,2,0:T(4,128)S(1)}, ...), condition=%wide.region_5.6_spmd, body=%wide.region_0.5_spmd.sunk | while | flops 1261904640 | bytes 71387728 | solution.py:81
  28.7 2.7 collective-permute-start
  37.6 35.6 %conditional.8 = ((f32[8,384,4]{1,2,0:T(4,128)S(1)}, f32[8,384,4]{1,2,0:T(4,128)S(1)}, f32[8,384,4,64]{1,3,2,0:T(8,128)})) conditional(s32[]{:T(128)} %convert_element_type.129, (f32[8,384,4]{1,2,0:T(4,128)S(1)}, f32[8,384,4]{1,2,0:T(4,128)S(1)}, f32[8,384,4,64]{1,3,2,0:T(8,128)}) %tuple.136, (s32[384]{0:T(512)S(1)}, s32[384]{0:T(512)}, s32[]{:T(128)}, ...), branch_computations={%region_1.1_spmd, %region_2.4_spmd} | conditional | flops 1261904640 | bytes 66659380 | solution.py:69
  38.5 10.6 %fusion = (f32[8,384,4]{1,2,0:T(4,128)S(1)}, f32[8,384,4,384]{1,3,2,0:T(8,128)}) fusion(pred[384,384]{0,1:T(8,128)(4,1)S(1)} %compare_and_fusion, bf16[384,8,4,64]{0,3,2,1:T(8,128)(2,1)} %get-tuple-element.722, bf16[384,8,64]{0,2,1:T(8,128)(2,1)} %get-tuple-element.723), kind=kOutput, calls=%fused_computation.2 | convolution fusion | flops 618123264 | bytes 21037056 | tf_op jit(solution)/shard_map/while/body/eval_jaxpr/cond/branch_1_fun/qkgd,skd->kqgs/dot_general | solution.py:19
  49.1 10.2 %fusion.2 = f32[8,384,4]{1,2,0:T(4,128)S(1)} fusion(f32[8,384,4,384]{1,3,2,0:T(8,128)} %get-tuple-element.924, f32[8,384,4]{1,2,0:T(4,128)S(1)} %max.4, pred[384,384]{0,1:T(8,128)(4,1)S(1)} %compare_and_fusion), kind=kLoop, calls=%fused_computation.4 | loop fusion | flops 18862080 | bytes 19120128 | tf_op jit(solution)/shard_map/while/body/eval_jaxpr/cond/branch_1_fun/reduce_sum | solution.py:24
  59.4 13.8 %multiply_add_fusion = f32[8,384,4,64]{1,3,2,0:T(8,128)} fusion(f32[8,384,4,64]{1,3,2,0:T(8,128)} %get-tuple-element.725, f32[8,384,4,384]{1,3,2,0:T(8,128)} %get-tuple-element.924, f32[8,384,4]{1,2,0:T(4,128)S(1)} %max.4, pred[384,384]{0,1:T(8,128)(4,1)S(1)} %compare_and_fusion, f32[8,384,4]{1,2,0:T(4,128)S(1)} %bitcast.190, ...), kind=kOutput, calls=%fused_computation.7 | convolution fusion | flops 624427008 | bytes 25804800 | tf_op jit(solution)/shard_map/while/body/eval_jaxpr/cond/branch_1_fun/kqgs,skd->kqgd/dot_general | solution.py:25
  80.0 35.6 %conditional.8 = ((f32[8,384,4]{1,2,0:T(4,128)S(1)}, f32[8,384,4]{1,2,0:T(4,128)S(1)}, f32[8,384,4,64]{1,3,2,0:T(8,128)})) conditional(s32[]{:T(128)} %convert_element_type.129, (f32[8,384,4]{1,2,0:T(4,128)S(1)}, f32[8,384,4]{1,2,0:T(4,128)S(1)}, f32[8,384,4,64]{1,3,2,0:T(8,128)}) %tuple.136, (s32[384]{0:T(512)S(1)}, s32[384]{0:T(512)}, s32[]{:T(128)}, ...), branch_computations={%region_1.1_spmd, %region_2.4_spmd} | conditional | flops 1261904640 | bytes 66659380 | solution.py:69
  80.9 10.6 %fusion = (f32[8,384,4]{1,2,0:T(4,128)S(1)}, f32[8,384,4,384]{1,3,2,0:T(8,128)}) fusion(pred[384,384]{0,1:T(8,128)(4,1)S(1)} %compare_and_fusion, bf16[384,8,4,64]{0,3,2,1:T(8,128)(2,1)} %get-tuple-element.722, bf16[384,8,64]{0,2,1:T(8,128)(2,1)} %get-tuple-element.723), kind=kOutput, calls=%fused_computation.2 | convolution fusion | flops 618123264 | bytes 21037056 | tf_op jit(solution)/shard_map/while/body/eval_jaxpr/cond/branch_1_fun/qkgd,skd->kqgs/dot_general | solution.py:19
  91.5 10.2 %fusion.2 = f32[8,384,4]{1,2,0:T(4,128)S(1)} fusion(f32[8,384,4,384]{1,3,2,0:T(8,128)} %get-tuple-element.924, f32[8,384,4]{1,2,0:T(4,128)S(1)} %max.4, pred[384,384]{0,1:T(8,128)(4,1)S(1)} %compare_and_fusion), kind=kLoop, calls=%fused_computation.4 | loop fusion | flops 18862080 | bytes 19120128 | tf_op jit(solution)/shard_map/while/body/eval_jaxpr/cond/branch_1_fun/reduce_sum | solution.py:24
  101.7 13.8 %multiply_add_fusion = f32[8,384,4,64]{1,3,2,0:T(8,128)} fusion(f32[8,384,4,64]{1,3,2,0:T(8,128)} %get-tuple-element.725, f32[8,384,4,384]{1,3,2,0:T(8,128)} %get-tuple-element.924, f32[8,384,4]{1,2,0:T(4,128)S(1)} %max.4, pred[384,384]{0,1:T(8,128)(4,1)S(1)} %compare_and_fusion, f32[8,384,4]{1,2,0:T(4,128)S(1)} %bitcast.190, ...), kind=kOutput, calls=%fused_computation.7 | convolution fusion | flops 624427008 | bytes 25804800 | tf_op jit(solution)/shard_map/while/body/eval_jaxpr/cond/branch_1_fun/kqgs,skd->kqgd/dot_general | solution.py:25
  122.8 3.2 collective-permute-done.2
  126.8 32.4 %collective-permute-start = (bf16[384,8,64]{0,2,1:T(8,128)(2,1)}, bf16[384,8,64]{0,2,1:T(8,128)(2,1)S(1)}, u32[]{:S(2)}, u32[]{:S(2)}) collective-permute-start(bf16[384,8,64]{0,2,1:T(8,128)(2,1)} %copy.76), channel_id=1, source_target_pairs={{0,1},{1,2},{2,3},{3,4},{4,5},{5,6},{6,7},{7,0},{8,9},{9,10},{10,1... | collective-permute-start | bytes 1179656 | tf_op jit(solution)/shard_map/while/body/eval_jaxpr/ppermute | solution.py:75
  172.1 30.5 %collective-permute-start.1 = (bf16[384,8,64]{0,2,1:T(8,128)(2,1)}, bf16[384,8,64]{0,2,1:T(8,128)(2,1)S(1)}, u32[]{:S(2)}, u32[]{:S(2)}) collective-permute-start(bf16[384,8,64]{0,2,1:T(8,128)(2,1)} %copy.77), channel_id=1, source_target_pairs={{0,1},{1,2},{2,3},{3,4},{4,5},{5,6},{6,7},{7,0},{8,9},{9,10},{10,1... | collective-permute-start | bytes 1179656 | tf_op jit(solution)/shard_map/while/body/eval_jaxpr/ppermute | solution.py:75
  233.7 9.6 bitcast_convert_fusion.1
  243.7 4.3 fusion.66
  251.0 369.2 %while.51 = (s32[]{:T(128)}, f32[8,384,4,64]{1,3,2,0:T(8,128)}, f32[8,384,64]{1,2,0:T(8,128)S(1)}, f32[8,384,64]{1,2,0:T(8,128)}, bf16[384,8,64]{0,2,1:T(8,128)(...) while((s32[]{:T(128)}, f32[8,384,4,64]{1,3,2,0:T(8,128)}, ...), condition=%wide.region_13.14_spmd, body=%wide.region_10.13_spmd.sunk | while | flops 3068707584 | bytes 129190656 | solution.py:111
  256.2 36.2 %conditional.9 = ((f32[8,384,4,64]{1,3,2,0:T(8,128)}, f32[8,384,64]{1,2,0:T(8,128)S(1)}, f32[8,384,64]{1,2,0:T(8,128)})) conditional(s32[]{:T(128)} %convert_element_type.130, (f32[8,384,4,64]{1,3,2,0:T(8,128)}, f32[8,384,64]{1,2,0:T(8,128)S(1)}, f32[8,384,64]{1,2,0:T(8,128)}) %tuple.139, (s32[384]{0:T(512)S(1)}, s32[384]{0:T(512)S(1)}, ...), branch_computations={%region_11.11_spmd, %region_12.12_spmd} | conditional | flops 3068707584 | bytes 115025000 | solution.py:100
  256.4 4.2 fusion.26
  260.6 6.8 fusion.21
  267.5 10.3 %multiply_convert_fusion = bf16[8,384,4,384]{3,1,2,0:T(8,128)(2,1)} fusion(f32[8,384,4,384]{3,1,2,0:T(8,128)S(1)} %fusion.26, f32[8,384,4]{1,2,0:T(4,128)S(1)} %get-tuple-element.762, f32[8,384,4]{1,2,0:T(4,128)S(1)} %get-tuple-element.759, pred[384,384]{1,0:T(8,128)(4,1)S(1)} %compare_and_fusion.1, bf16[384,8,4,64]{0,3,2,1:T(8,128)(2,1)} %get-tuple-element.760, ...), kind=kOutput, calls=%fused_computation.18 | convolution fusion | flops 632291328 | bytes 30523392 | tf_op jit(solution)/shard_map/while/body/eval_jaxpr/cond/branch_1_fun/qkgd,skd->kqgs/dot_general | solution.py:32
  277.8 5.4 fusion.20
  283.1 9.3 convolution_add_fusion
  298.4 5.4 collective-permute-done.3
  305.0 7.3 collective-permute-done.4
  314.3 6.4 collective-permute-done.7
  325.9 36.2 %conditional.9 = ((f32[8,384,4,64]{1,3,2,0:T(8,128)}, f32[8,384,64]{1,2,0:T(8,128)S(1)}, f32[8,384,64]{1,2,0:T(8,128)})) conditional(s32[]{:T(128)} %convert_element_type.130, (f32[8,384,4,64]{1,3,2,0:T(8,128)}, f32[8,384,64]{1,2,0:T(8,128)S(1)}, f32[8,384,64]{1,2,0:T(8,128)}) %tuple.139, (s32[384]{0:T(512)S(1)}, s32[384]{0:T(512)S(1)}, ...), branch_computations={%region_11.11_spmd, %region_12.12_spmd} | conditional | flops 3068707584 | bytes 115025000 | solution.py:100
  326.1 4.2 fusion.26
  330.3 6.8 fusion.21
  337.1 10.3 %multiply_convert_fusion = bf16[8,384,4,384]{3,1,2,0:T(8,128)(2,1)} fusion(f32[8,384,4,384]{3,1,2,0:T(8,128)S(1)} %fusion.26, f32[8,384,4]{1,2,0:T(4,128)S(1)} %get-tuple-element.762, f32[8,384,4]{1,2,0:T(4,128)S(1)} %get-tuple-element.759, pred[384,384]{1,0:T(8,128)(4,1)S(1)} %compare_and_fusion.1, bf16[384,8,4,64]{0,3,2,1:T(8,128)(2,1)} %get-tuple-element.760, ...), kind=kOutput, calls=%fused_computation.18 | convolution fusion | flops 632291328 | bytes 30523392 | tf_op jit(solution)/shard_map/while/body/eval_jaxpr/cond/branch_1_fun/qkgd,skd->kqgs/dot_general | solution.py:32
  347.4 5.4 fusion.20
  352.8 9.3 convolution_add_fusion
  368.1 5.4 collective-permute-done.3
  374.6 7.3 collective-permute-done.4
  384.0 6.4 collective-permute-done.7
  395.6 38.7 %collective-permute-start.3 = (f32[8,384,64]{1,2,0:T(8,128)S(1)}, f32[8,384,64]{1,2,0:T(8,128)}, u32[]{:S(2)}, u32[]{:S(2)}) collective-permute-start(f32[8,384,64]{1,2,0:T(8,128)S(1)} %get-tuple-element.1098), channel_id=1, source_target_pairs={{0,1},{1,2},{2,3},{3,4},{4,5},{5,6},{6,7},{7,0},{8,9},{9,10},{10,1... | collective-permute-start | bytes 2359304 | tf_op jit(solution)/shard_map/while/body/eval_jaxpr/ppermute | solution.py:106
  435.3 7.8 collective-permute-done.3
  444.3 7.3 collective-permute-done.4
  453.6 6.4 collective-permute-done.7
  467.7 34.6 %collective-permute-start.4 = (f32[8,384,64]{1,2,0:T(8,128)}, f32[8,384,64]{1,2,0:T(8,128)}, u32[]{:S(2)}, u32[]{:S(2)}) collective-permute-start(f32[8,384,64]{1,2,0:T(8,128)} %get-tuple-element.1099), channel_id=1, source_target_pairs={{0,1},{1,2},{2,3},{3,4},{4,5},{5,6},{6,7},{7,0},{8,9},{9,10},{10,1... | collective-permute-start | bytes 2359304 | tf_op jit(solution)/shard_map/while/body/eval_jaxpr/ppermute | solution.py:106
  503.6 7.7 collective-permute-done.4
  513.3 6.4 collective-permute-done.7
  527.4 5.9 collective-permute-start.4
  537.5 7.3 collective-permute-done.4
  546.8 6.4 collective-permute-done.7
  560.9 5.9 collective-permute-start.4
  571.0 7.3 collective-permute-done.4
  580.3 6.4 collective-permute-done.7
  594.4 5.9 collective-permute-start.4
  604.4 7.3 collective-permute-done.4
  613.8 6.4 collective-permute-done.7
  626.0 4.7 collective-permute-done.9
  630.7 4.7 convolution_bitcast_fusion.2
  638.3 8.9 collective-permute-done.8
  648.1 4.7 convolution_bitcast_fusion.3
  653.0 12.6 %fusion.71 = f32[8,4,64,2048]{3,2,1,0:T(8,128)} fusion(bf16[384,2048]{1,0:T(8,128)(2,1)} %param.19, f32[8,384,4,64]{1,3,2,0:T(8,128)} %get-tuple-element.835), kind=kOutput, calls=%fused_computation.92 | convolution fusion | flops 3222798336 | bytes 21495808 | tf_op jit(solution)/shard_map/qm,kqgd->mkgd/dot_general | solution.py:123
  665.7 12.1 %fusion.69 = f32[8,4,64,2048]{3,2,1,0:T(8,128)} fusion(bf16[8,384,4,64]{1,3,2,0:T(8,128)(2,1)} %get-tuple-element.918, bf16[384,2048]{1,0:T(8,128)(2,1)} %param.25), kind=kOutput, calls=%fused_computation.90 | convolution fusion | flops 3221225472 | bytes 19922944 | tf_op jit(solution)/shard_map/qm,kqgd->mkgd/dot_general | solution.py:89
  677.9 8.5 bitcast_convert_fusion
  686.4 6.9 fusion.60
  697.2 41.8 %reduce-scatter.9.cloned.1.call-done = f32[256,8,64]{0,2,1:T(8,128)} async-done(((f32[2048,8,64]{0,2,1:T(8,128)}), f32[256,8,64]{0,2,1:T(8,128)}) %reduce-scatter.9.cloned.1.call-update) | async-done | bytes 524304 | tf_op jit(solution)/shard_map/reduce_scatter | solution.py:128
  739.0 37.8 %reduce-scatter.7.cloned.1.call-done = f32[256,8,64]{0,2,1:T(8,128)} async-done(((f32[2048,8,64]{0,2,1:T(8,128)}), f32[256,8,64]{0,2,1:T(8,128)}) %reduce-scatter.7.cloned.1.call-update) | async-done | bytes 524304 | tf_op jit(solution)/shard_map/reduce_scatter | solution.py:128
  776.8 93.0 %reduce-scatter.5.cloned.1.call-done = f32[256,32,64]{0,2,1:T(8,128)} async-done(((f32[2048,32,64]{0,2,1:T(8,128)}), f32[256,32,64]{0,2,1:T(8,128)}) %reduce-scatter.5.cloned.1.call-update) | async-done | bytes 2097168 | tf_op jit(solution)/shard_map/reduce_scatter | solution.py:128
  869.7 91.2 %reduce-scatter.11.cloned.1.call-done = f32[256,32,64]{0,2,1:T(8,128)} async-done(((f32[2048,32,64]{0,2,1:T(8,128)}), f32[256,32,64]{0,2,1:T(8,128)}) %reduce-scatter.11.cloned.1.call-update) | async-done | bytes 2097168 | tf_op jit(solution)/shard_map/reduce_scatter | solution.py:128
  (251 shorter events, 167.3 us)
Async XLA Ops:
  7.2 731.8 %reduce-scatter.9.cloned.1.call-start = ((), (), s32[]{:S(2)}) async-start(), calls=%async_computation.6 | async-start | bytes 4718592 | tf_op jit(solution)/shard_map/reduce_scatter | solution.py:128
  28.7 44.5 %collective-permute-start = (bf16[384,8,64]{0,2,1:T(8,128)(2,1)}, bf16[384,8,64]{0,2,1:T(8,128)(2,1)S(1)}, u32[]{:S(2)}, u32[]{:S(2)}) collective-permute-start(bf16[384,8,64]{0,2,1:T(8,128)(2,1)} %copy.76), channel_id=1, source_target_pairs={{0,1},{1,2},{2,3},{3,4},{4,5},{5,6},{6,7},{7,0},{8,9},{9,10},{10,1... | collective-permute-start | bytes 1179656 | tf_op jit(solution)/shard_map/while/body/eval_jaxpr/ppermute | solution.py:75
  32.1 41.1 %collective-permute-start.1 = (bf16[384,8,64]{0,2,1:T(8,128)(2,1)}, bf16[384,8,64]{0,2,1:T(8,128)(2,1)S(1)}, u32[]{:S(2)}, u32[]{:S(2)}) collective-permute-start(bf16[384,8,64]{0,2,1:T(8,128)(2,1)} %copy.77), channel_id=1, source_target_pairs={{0,1},{1,2},{2,3},{3,4},{4,5},{5,6},{6,7},{7,0},{8,9},{9,10},{10,1... | collective-permute-start | bytes 1179656 | tf_op jit(solution)/shard_map/while/body/eval_jaxpr/ppermute | solution.py:75
  32.7 40.5 %collective-permute-start.2 = (s32[384]{0:T(512)}, s32[384]{0:T(512)S(1)}, u32[]{:S(2)}, u32[]{:S(2)}) collective-permute-start(s32[384]{0:T(512)} %copy.78), channel_id=1, source_target_pairs={{0,1},{1,2},{2,3},{3,4},{4,5},{5,6},{6,7},{7,0},{8,9},{9,10},{10,1... | collective-permute-start | bytes 4616 | tf_op jit(solution)/shard_map/while/body/eval_jaxpr/ppermute | solution.py:75
  74.0 41.6 %collective-permute-start = (bf16[384,8,64]{0,2,1:T(8,128)(2,1)}, bf16[384,8,64]{0,2,1:T(8,128)(2,1)S(1)}, u32[]{:S(2)}, u32[]{:S(2)}) collective-permute-start(bf16[384,8,64]{0,2,1:T(8,128)(2,1)} %copy.76), channel_id=1, source_target_pairs={{0,1},{1,2},{2,3},{3,4},{4,5},{5,6},{6,7},{7,0},{8,9},{9,10},{10,1... | collective-permute-start | bytes 1179656 | tf_op jit(solution)/shard_map/while/body/eval_jaxpr/ppermute | solution.py:75
  74.7 40.8 %collective-permute-start.1 = (bf16[384,8,64]{0,2,1:T(8,128)(2,1)}, bf16[384,8,64]{0,2,1:T(8,128)(2,1)S(1)}, u32[]{:S(2)}, u32[]{:S(2)}) collective-permute-start(bf16[384,8,64]{0,2,1:T(8,128)(2,1)} %copy.77), channel_id=1, source_target_pairs={{0,1},{1,2},{2,3},{3,4},{4,5},{5,6},{6,7},{7,0},{8,9},{9,10},{10,1... | collective-permute-start | bytes 1179656 | tf_op jit(solution)/shard_map/while/body/eval_jaxpr/ppermute | solution.py:75
  76.8 38.8 %collective-permute-start.2 = (s32[384]{0:T(512)}, s32[384]{0:T(512)S(1)}, u32[]{:S(2)}, u32[]{:S(2)}) collective-permute-start(s32[384]{0:T(512)} %copy.78), channel_id=1, source_target_pairs={{0,1},{1,2},{2,3},{3,4},{4,5},{5,6},{6,7},{7,0},{8,9},{9,10},{10,1... | collective-permute-start | bytes 4616 | tf_op jit(solution)/shard_map/while/body/eval_jaxpr/ppermute | solution.py:75
  116.3 9.7 %collective-permute-start = (bf16[384,8,64]{0,2,1:T(8,128)(2,1)}, bf16[384,8,64]{0,2,1:T(8,128)(2,1)S(1)}, u32[]{:S(2)}, u32[]{:S(2)}) collective-permute-start(bf16[384,8,64]{0,2,1:T(8,128)(2,1)} %copy.76), channel_id=1, source_target_pairs={{0,1},{1,2},{2,3},{3,4},{4,5},{5,6},{6,7},{7,0},{8,9},{9,10},{10,1... | collective-permute-start | bytes 1179656 | tf_op jit(solution)/shard_map/while/body/eval_jaxpr/ppermute | solution.py:75
  117.9 8.2 collective-permute-start.1
  118.4 7.6 collective-permute-start.2
  126.8 41.3 %collective-permute-start = (bf16[384,8,64]{0,2,1:T(8,128)(2,1)}, bf16[384,8,64]{0,2,1:T(8,128)(2,1)S(1)}, u32[]{:S(2)}, u32[]{:S(2)}) collective-permute-start(bf16[384,8,64]{0,2,1:T(8,128)(2,1)} %copy.76), channel_id=1, source_target_pairs={{0,1},{1,2},{2,3},{3,4},{4,5},{5,6},{6,7},{7,0},{8,9},{9,10},{10,1... | collective-permute-start | bytes 1179656 | tf_op jit(solution)/shard_map/while/body/eval_jaxpr/ppermute | solution.py:75
  159.9 8.2 collective-permute-start.1
  162.2 5.9 collective-permute-start.2
  168.9 38.4 %collective-permute-start = (bf16[384,8,64]{0,2,1:T(8,128)(2,1)}, bf16[384,8,64]{0,2,1:T(8,128)(2,1)S(1)}, u32[]{:S(2)}, u32[]{:S(2)}) collective-permute-start(bf16[384,8,64]{0,2,1:T(8,128)(2,1)} %copy.76), channel_id=1, source_target_pairs={{0,1},{1,2},{2,3},{3,4},{4,5},{5,6},{6,7},{7,0},{8,9},{9,10},{10,1... | collective-permute-start | bytes 1179656 | tf_op jit(solution)/shard_map/while/body/eval_jaxpr/ppermute | solution.py:75
  172.1 35.2 %collective-permute-start.1 = (bf16[384,8,64]{0,2,1:T(8,128)(2,1)}, bf16[384,8,64]{0,2,1:T(8,128)(2,1)S(1)}, u32[]{:S(2)}, u32[]{:S(2)}) collective-permute-start(bf16[384,8,64]{0,2,1:T(8,128)(2,1)} %copy.77), channel_id=1, source_target_pairs={{0,1},{1,2},{2,3},{3,4},{4,5},{5,6},{6,7},{7,0},{8,9},{9,10},{10,1... | collective-permute-start | bytes 1179656 | tf_op jit(solution)/shard_map/while/body/eval_jaxpr/ppermute | solution.py:75
  203.2 4.1 collective-permute-start.2
  208.0 11.4 %collective-permute-start = (bf16[384,8,64]{0,2,1:T(8,128)(2,1)}, bf16[384,8,64]{0,2,1:T(8,128)(2,1)S(1)}, u32[]{:S(2)}, u32[]{:S(2)}) collective-permute-start(bf16[384,8,64]{0,2,1:T(8,128)(2,1)} %copy.76), channel_id=1, source_target_pairs={{0,1},{1,2},{2,3},{3,4},{4,5},{5,6},{6,7},{7,0},{8,9},{9,10},{10,1... | collective-permute-start | bytes 1179656 | tf_op jit(solution)/shard_map/while/body/eval_jaxpr/ppermute | solution.py:75
  211.3 8.2 collective-permute-start.1
  212.8 6.6 collective-permute-start.2
  220.2 11.4 %collective-permute-start = (bf16[384,8,64]{0,2,1:T(8,128)(2,1)}, bf16[384,8,64]{0,2,1:T(8,128)(2,1)S(1)}, u32[]{:S(2)}, u32[]{:S(2)}) collective-permute-start(bf16[384,8,64]{0,2,1:T(8,128)(2,1)} %copy.76), channel_id=1, source_target_pairs={{0,1},{1,2},{2,3},{3,4},{4,5},{5,6},{6,7},{7,0},{8,9},{9,10},{10,1... | collective-permute-start | bytes 1179656 | tf_op jit(solution)/shard_map/while/body/eval_jaxpr/ppermute | solution.py:75
  223.5 8.2 collective-permute-start.1
  225.0 6.6 collective-permute-start.2
  267.5 10.3 %copy-start.1 = (bf16[384,8,4,64]{0,3,2,1:T(8,128)(2,1)S(1)}, bf16[384,8,4,64]{0,3,2,1:T(8,128)(2,1)}, u32[]{:S(2)}) copy-start(bf16[384,8,4,64]{0,3,2,1:T(8,128)(2,1)} %get-tuple-element.757) | copy-start | bytes 4718596 | tf_op jit(solution)/shard_map/while/body/eval_jaxpr/cond
  292.4 11.4 %collective-permute-start.3 = (f32[8,384,64]{1,2,0:T(8,128)S(1)}, f32[8,384,64]{1,2,0:T(8,128)}, u32[]{:S(2)}, u32[]{:S(2)}) collective-permute-start(f32[8,384,64]{1,2,0:T(8,128)S(1)} %get-tuple-element.1098), channel_id=1, source_target_pairs={{0,1},{1,2},{2,3},{3,4},{4,5},{5,6},{6,7},{7,0},{8,9},{9,10},{10,1... | collective-permute-start | bytes 2359304 | tf_op jit(solution)/shard_map/while/body/eval_jaxpr/ppermute | solution.py:106
  294.9 17.3 %collective-permute-start.4 = (f32[8,384,64]{1,2,0:T(8,128)}, f32[8,384,64]{1,2,0:T(8,128)}, u32[]{:S(2)}, u32[]{:S(2)}) collective-permute-start(f32[8,384,64]{1,2,0:T(8,128)} %get-tuple-element.1099), channel_id=1, source_target_pairs={{0,1},{1,2},{2,3},{3,4},{4,5},{5,6},{6,7},{7,0},{8,9},{9,10},{10,1... | collective-permute-start | bytes 2359304 | tf_op jit(solution)/shard_map/while/body/eval_jaxpr/ppermute | solution.py:106
  295.9 24.8 %collective-permute-start.5 = (bf16[384,8,64]{0,2,1:T(8,128)(2,1)S(1)}, bf16[384,8,64]{0,2,1:T(8,128)(2,1)}, u32[]{:S(2)}, u32[]{:S(2)}) collective-permute-start(bf16[384,8,64]{0,2,1:T(8,128)(2,1)S(1)} %copy.103), channel_id=1, source_target_pairs={{0,1},{1,2},{2,3},{3,4},{4,5},{5,6},{6,7},{7,0},{8,9},{9,10},{10,1... | collective-permute-start | bytes 1179656 | tf_op jit(solution)/shard_map/while/body/eval_jaxpr/ppermute | solution.py:106
  298.4 22.3 %collective-permute-start.6 = (bf16[384,8,64]{0,2,1:T(8,128)(2,1)}, bf16[384,8,64]{0,2,1:T(8,128)(2,1)}, u32[]{:S(2)}, u32[]{:S(2)}) collective-permute-start(bf16[384,8,64]{0,2,1:T(8,128)(2,1)} %copy.104), channel_id=1, source_target_pairs={{0,1},{1,2},{2,3},{3,4},{4,5},{5,6},{6,7},{7,0},{8,9},{9,10},{10,1... | collective-permute-start | bytes 1179656 | tf_op jit(solution)/shard_map/while/body/eval_jaxpr/ppermute | solution.py:106
  298.4 22.3 %collective-permute-start.7 = (s32[384]{0:T(512)S(1)}, s32[384]{0:T(512)S(1)}, u32[]{:S(2)}, u32[]{:S(2)}) collective-permute-start(s32[384]{0:T(512)S(1)} %copy.105), channel_id=1, source_target_pairs={{0,1},{1,2},{2,3},{3,4},{4,5},{5,6},{6,7},{7,0},{8,9},{9,10},{10,1... | collective-permute-start | bytes 4616 | tf_op jit(solution)/shard_map/while/body/eval_jaxpr/ppermute | solution.py:106
  337.1 10.3 %copy-start.1 = (bf16[384,8,4,64]{0,3,2,1:T(8,128)(2,1)S(1)}, bf16[384,8,4,64]{0,3,2,1:T(8,128)(2,1)}, u32[]{:S(2)}) copy-start(bf16[384,8,4,64]{0,3,2,1:T(8,128)(2,1)} %get-tuple-element.757) | copy-start | bytes 4718596 | tf_op jit(solution)/shard_map/while/body/eval_jaxpr/cond
  362.1 11.4 %collective-permute-start.3 = (f32[8,384,64]{1,2,0:T(8,128)S(1)}, f32[8,384,64]{1,2,0:T(8,128)}, u32[]{:S(2)}, u32[]{:S(2)}) collective-permute-start(f32[8,384,64]{1,2,0:T(8,128)S(1)} %get-tuple-element.1098), channel_id=1, source_target_pairs={{0,1},{1,2},{2,3},{3,4},{4,5},{5,6},{6,7},{7,0},{8,9},{9,10},{10,1... | collective-permute-start | bytes 2359304 | tf_op jit(solution)/shard_map/while/body/eval_jaxpr/ppermute | solution.py:106
  364.6 17.3 %collective-permute-start.4 = (f32[8,384,64]{1,2,0:T(8,128)}, f32[8,384,64]{1,2,0:T(8,128)}, u32[]{:S(2)}, u32[]{:S(2)}) collective-permute-start(f32[8,384,64]{1,2,0:T(8,128)} %get-tuple-element.1099), channel_id=1, source_target_pairs={{0,1},{1,2},{2,3},{3,4},{4,5},{5,6},{6,7},{7,0},{8,9},{9,10},{10,1... | collective-permute-start | bytes 2359304 | tf_op jit(solution)/shard_map/while/body/eval_jaxpr/ppermute | solution.py:106
  365.5 24.8 %collective-permute-start.5 = (bf16[384,8,64]{0,2,1:T(8,128)(2,1)S(1)}, bf16[384,8,64]{0,2,1:T(8,128)(2,1)}, u32[]{:S(2)}, u32[]{:S(2)}) collective-permute-start(bf16[384,8,64]{0,2,1:T(8,128)(2,1)S(1)} %copy.103), channel_id=1, source_target_pairs={{0,1},{1,2},{2,3},{3,4},{4,5},{5,6},{6,7},{7,0},{8,9},{9,10},{10,1... | collective-permute-start | bytes 1179656 | tf_op jit(solution)/shard_map/while/body/eval_jaxpr/ppermute | solution.py:106
  368.0 22.3 %collective-permute-start.6 = (bf16[384,8,64]{0,2,1:T(8,128)(2,1)}, bf16[384,8,64]{0,2,1:T(8,128)(2,1)}, u32[]{:S(2)}, u32[]{:S(2)}) collective-permute-start(bf16[384,8,64]{0,2,1:T(8,128)(2,1)} %copy.104), channel_id=1, source_target_pairs={{0,1},{1,2},{2,3},{3,4},{4,5},{5,6},{6,7},{7,0},{8,9},{9,10},{10,1... | collective-permute-start | bytes 1179656 | tf_op jit(solution)/shard_map/while/body/eval_jaxpr/ppermute | solution.py:106
  368.1 22.3 %collective-permute-start.7 = (s32[384]{0:T(512)S(1)}, s32[384]{0:T(512)S(1)}, u32[]{:S(2)}, u32[]{:S(2)}) collective-permute-start(s32[384]{0:T(512)S(1)} %copy.105), channel_id=1, source_target_pairs={{0,1},{1,2},{2,3},{3,4},{4,5},{5,6},{6,7},{7,0},{8,9},{9,10},{10,1... | collective-permute-start | bytes 4616 | tf_op jit(solution)/shard_map/while/body/eval_jaxpr/ppermute | solution.py:106
  395.6 47.6 %collective-permute-start.3 = (f32[8,384,64]{1,2,0:T(8,128)S(1)}, f32[8,384,64]{1,2,0:T(8,128)}, u32[]{:S(2)}, u32[]{:S(2)}) collective-permute-start(f32[8,384,64]{1,2,0:T(8,128)S(1)} %get-tuple-element.1098), channel_id=1, source_target_pairs={{0,1},{1,2},{2,3},{3,4},{4,5},{5,6},{6,7},{7,0},{8,9},{9,10},{10,1... | collective-permute-start | bytes 2359304 | tf_op jit(solution)/shard_map/while/body/eval_jaxpr/ppermute | solution.py:106
  434.2 17.3 %collective-permute-start.4 = (f32[8,384,64]{1,2,0:T(8,128)}, f32[8,384,64]{1,2,0:T(8,128)}, u32[]{:S(2)}, u32[]{:S(2)}) collective-permute-start(f32[8,384,64]{1,2,0:T(8,128)} %get-tuple-element.1099), channel_id=1, source_target_pairs={{0,1},{1,2},{2,3},{3,4},{4,5},{5,6},{6,7},{7,0},{8,9},{9,10},{10,1... | collective-permute-start | bytes 2359304 | tf_op jit(solution)/shard_map/while/body/eval_jaxpr/ppermute | solution.py:106
  435.2 24.8 %collective-permute-start.5 = (bf16[384,8,64]{0,2,1:T(8,128)(2,1)S(1)}, bf16[384,8,64]{0,2,1:T(8,128)(2,1)}, u32[]{:S(2)}, u32[]{:S(2)}) collective-permute-start(bf16[384,8,64]{0,2,1:T(8,128)(2,1)S(1)} %copy.103), channel_id=1, source_target_pairs={{0,1},{1,2},{2,3},{3,4},{4,5},{5,6},{6,7},{7,0},{8,9},{9,10},{10,1... | collective-permute-start | bytes 1179656 | tf_op jit(solution)/shard_map/while/body/eval_jaxpr/ppermute | solution.py:106
  435.2 24.8 %collective-permute-start.6 = (bf16[384,8,64]{0,2,1:T(8,128)(2,1)}, bf16[384,8,64]{0,2,1:T(8,128)(2,1)}, u32[]{:S(2)}, u32[]{:S(2)}) collective-permute-start(bf16[384,8,64]{0,2,1:T(8,128)(2,1)} %copy.104), channel_id=1, source_target_pairs={{0,1},{1,2},{2,3},{3,4},{4,5},{5,6},{6,7},{7,0},{8,9},{9,10},{10,1... | collective-permute-start | bytes 1179656 | tf_op jit(solution)/shard_map/while/body/eval_jaxpr/ppermute | solution.py:106
  435.2 24.8 %collective-permute-start.7 = (s32[384]{0:T(512)S(1)}, s32[384]{0:T(512)S(1)}, u32[]{:S(2)}, u32[]{:S(2)}) collective-permute-start(s32[384]{0:T(512)S(1)} %copy.105), channel_id=1, source_target_pairs={{0,1},{1,2},{2,3},{3,4},{4,5},{5,6},{6,7},{7,0},{8,9},{9,10},{10,1... | collective-permute-start | bytes 4616 | tf_op jit(solution)/shard_map/while/body/eval_jaxpr/ppermute | solution.py:106
  465.2 37.3 %collective-permute-start.3 = (f32[8,384,64]{1,2,0:T(8,128)S(1)}, f32[8,384,64]{1,2,0:T(8,128)}, u32[]{:S(2)}, u32[]{:S(2)}) collective-permute-start(f32[8,384,64]{1,2,0:T(8,128)S(1)} %get-tuple-element.1098), channel_id=1, source_target_pairs={{0,1},{1,2},{2,3},{3,4},{4,5},{5,6},{6,7},{7,0},{8,9},{9,10},{10,1... | collective-permute-start | bytes 2359304 | tf_op jit(solution)/shard_map/while/body/eval_jaxpr/ppermute | solution.py:106
  467.7 43.6 %collective-permute-start.4 = (f32[8,384,64]{1,2,0:T(8,128)}, f32[8,384,64]{1,2,0:T(8,128)}, u32[]{:S(2)}, u32[]{:S(2)}) collective-permute-start(f32[8,384,64]{1,2,0:T(8,128)} %get-tuple-element.1099), channel_id=1, source_target_pairs={{0,1},{1,2},{2,3},{3,4},{4,5},{5,6},{6,7},{7,0},{8,9},{9,10},{10,1... | collective-permute-start | bytes 2359304 | tf_op jit(solution)/shard_map/while/body/eval_jaxpr/ppermute | solution.py:106
  502.4 17.4 %collective-permute-start.5 = (bf16[384,8,64]{0,2,1:T(8,128)(2,1)S(1)}, bf16[384,8,64]{0,2,1:T(8,128)(2,1)}, u32[]{:S(2)}, u32[]{:S(2)}) collective-permute-start(bf16[384,8,64]{0,2,1:T(8,128)(2,1)S(1)} %copy.103), channel_id=1, source_target_pairs={{0,1},{1,2},{2,3},{3,4},{4,5},{5,6},{6,7},{7,0},{8,9},{9,10},{10,1... | collective-permute-start | bytes 1179656 | tf_op jit(solution)/shard_map/while/body/eval_jaxpr/ppermute | solution.py:106
  502.4 17.3 %collective-permute-start.6 = (bf16[384,8,64]{0,2,1:T(8,128)(2,1)}, bf16[384,8,64]{0,2,1:T(8,128)(2,1)}, u32[]{:S(2)}, u32[]{:S(2)}) collective-permute-start(bf16[384,8,64]{0,2,1:T(8,128)(2,1)} %copy.104), channel_id=1, source_target_pairs={{0,1},{1,2},{2,3},{3,4},{4,5},{5,6},{6,7},{7,0},{8,9},{9,10},{10,1... | collective-permute-start | bytes 1179656 | tf_op jit(solution)/shard_map/while/body/eval_jaxpr/ppermute | solution.py:106
  502.4 17.3 %collective-permute-start.7 = (s32[384]{0:T(512)S(1)}, s32[384]{0:T(512)S(1)}, u32[]{:S(2)}, u32[]{:S(2)}) collective-permute-start(s32[384]{0:T(512)S(1)} %copy.105), channel_id=1, source_target_pairs={{0,1},{1,2},{2,3},{3,4},{4,5},{5,6},{6,7},{7,0},{8,9},{9,10},{10,1... | collective-permute-start | bytes 4616 | tf_op jit(solution)/shard_map/while/body/eval_jaxpr/ppermute | solution.py:106
  524.9 11.4 %collective-permute-start.3 = (f32[8,384,64]{1,2,0:T(8,128)S(1)}, f32[8,384,64]{1,2,0:T(8,128)}, u32[]{:S(2)}, u32[]{:S(2)}) collective-permute-start(f32[8,384,64]{1,2,0:T(8,128)S(1)} %get-tuple-element.1098), channel_id=1, source_target_pairs={{0,1},{1,2},{2,3},{3,4},{4,5},{5,6},{6,7},{7,0},{8,9},{9,10},{10,1... | collective-permute-start | bytes 2359304 | tf_op jit(solution)/shard_map/while/body/eval_jaxpr/ppermute | solution.py:106
  527.4 17.3 %collective-permute-start.4 = (f32[8,384,64]{1,2,0:T(8,128)}, f32[8,384,64]{1,2,0:T(8,128)}, u32[]{:S(2)}, u32[]{:S(2)}) collective-permute-start(f32[8,384,64]{1,2,0:T(8,128)} %get-tuple-element.1099), channel_id=1, source_target_pairs={{0,1},{1,2},{2,3},{3,4},{4,5},{5,6},{6,7},{7,0},{8,9},{9,10},{10,1... | collective-permute-start | bytes 2359304 | tf_op jit(solution)/shard_map/while/body/eval_jaxpr/ppermute | solution.py:106
  533.3 19.9 %collective-permute-start.5 = (bf16[384,8,64]{0,2,1:T(8,128)(2,1)S(1)}, bf16[384,8,64]{0,2,1:T(8,128)(2,1)}, u32[]{:S(2)}, u32[]{:S(2)}) collective-permute-start(bf16[384,8,64]{0,2,1:T(8,128)(2,1)S(1)} %copy.103), channel_id=1, source_target_pairs={{0,1},{1,2},{2,3},{3,4},{4,5},{5,6},{6,7},{7,0},{8,9},{9,10},{10,1... | collective-permute-start | bytes 1179656 | tf_op jit(solution)/shard_map/while/body/eval_jaxpr/ppermute | solution.py:106
  535.8 17.4 %collective-permute-start.6 = (bf16[384,8,64]{0,2,1:T(8,128)(2,1)}, bf16[384,8,64]{0,2,1:T(8,128)(2,1)}, u32[]{:S(2)}, u32[]{:S(2)}) collective-permute-start(bf16[384,8,64]{0,2,1:T(8,128)(2,1)} %copy.104), channel_id=1, source_target_pairs={{0,1},{1,2},{2,3},{3,4},{4,5},{5,6},{6,7},{7,0},{8,9},{9,10},{10,1... | collective-permute-start | bytes 1179656 | tf_op jit(solution)/shard_map/while/body/eval_jaxpr/ppermute | solution.py:106
  535.9 17.3 %collective-permute-start.7 = (s32[384]{0:T(512)S(1)}, s32[384]{0:T(512)S(1)}, u32[]{:S(2)}, u32[]{:S(2)}) collective-permute-start(s32[384]{0:T(512)S(1)} %copy.105), channel_id=1, source_target_pairs={{0,1},{1,2},{2,3},{3,4},{4,5},{5,6},{6,7},{7,0},{8,9},{9,10},{10,1... | collective-permute-start | bytes 4616 | tf_op jit(solution)/shard_map/while/body/eval_jaxpr/ppermute | solution.py:106
  558.4 11.4 %collective-permute-start.3 = (f32[8,384,64]{1,2,0:T(8,128)S(1)}, f32[8,384,64]{1,2,0:T(8,128)}, u32[]{:S(2)}, u32[]{:S(2)}) collective-permute-start(f32[8,384,64]{1,2,0:T(8,128)S(1)} %get-tuple-element.1098), channel_id=1, source_target_pairs={{0,1},{1,2},{2,3},{3,4},{4,5},{5,6},{6,7},{7,0},{8,9},{9,10},{10,1... | collective-permute-start | bytes 2359304 | tf_op jit(solution)/shard_map/while/body/eval_jaxpr/ppermute | solution.py:106
  560.9 17.3 %collective-permute-start.4 = (f32[8,384,64]{1,2,0:T(8,128)}, f32[8,384,64]{1,2,0:T(8,128)}, u32[]{:S(2)}, u32[]{:S(2)}) collective-permute-start(f32[8,384,64]{1,2,0:T(8,128)} %get-tuple-element.1099), channel_id=1, source_target_pairs={{0,1},{1,2},{2,3},{3,4},{4,5},{5,6},{6,7},{7,0},{8,9},{9,10},{10,1... | collective-permute-start | bytes 2359304 | tf_op jit(solution)/shard_map/while/body/eval_jaxpr/ppermute | solution.py:106
  566.8 19.9 %collective-permute-start.5 = (bf16[384,8,64]{0,2,1:T(8,128)(2,1)S(1)}, bf16[384,8,64]{0,2,1:T(8,128)(2,1)}, u32[]{:S(2)}, u32[]{:S(2)}) collective-permute-start(bf16[384,8,64]{0,2,1:T(8,128)(2,1)S(1)} %copy.103), channel_id=1, source_target_pairs={{0,1},{1,2},{2,3},{3,4},{4,5},{5,6},{6,7},{7,0},{8,9},{9,10},{10,1... | collective-permute-start | bytes 1179656 | tf_op jit(solution)/shard_map/while/body/eval_jaxpr/ppermute | solution.py:106
  569.3 17.4 %collective-permute-start.6 = (bf16[384,8,64]{0,2,1:T(8,128)(2,1)}, bf16[384,8,64]{0,2,1:T(8,128)(2,1)}, u32[]{:S(2)}, u32[]{:S(2)}) collective-permute-start(bf16[384,8,64]{0,2,1:T(8,128)(2,1)} %copy.104), channel_id=1, source_target_pairs={{0,1},{1,2},{2,3},{3,4},{4,5},{5,6},{6,7},{7,0},{8,9},{9,10},{10,1... | collective-permute-start | bytes 1179656 | tf_op jit(solution)/shard_map/while/body/eval_jaxpr/ppermute | solution.py:106
  569.4 17.3 %collective-permute-start.7 = (s32[384]{0:T(512)S(1)}, s32[384]{0:T(512)S(1)}, u32[]{:S(2)}, u32[]{:S(2)}) collective-permute-start(s32[384]{0:T(512)S(1)} %copy.105), channel_id=1, source_target_pairs={{0,1},{1,2},{2,3},{3,4},{4,5},{5,6},{6,7},{7,0},{8,9},{9,10},{10,1... | collective-permute-start | bytes 4616 | tf_op jit(solution)/shard_map/while/body/eval_jaxpr/ppermute | solution.py:106
  591.9 11.4 %collective-permute-start.3 = (f32[8,384,64]{1,2,0:T(8,128)S(1)}, f32[8,384,64]{1,2,0:T(8,128)}, u32[]{:S(2)}, u32[]{:S(2)}) collective-permute-start(f32[8,384,64]{1,2,0:T(8,128)S(1)} %get-tuple-element.1098), channel_id=1, source_target_pairs={{0,1},{1,2},{2,3},{3,4},{4,5},{5,6},{6,7},{7,0},{8,9},{9,10},{10,1... | collective-permute-start | bytes 2359304 | tf_op jit(solution)/shard_map/while/body/eval_jaxpr/ppermute | solution.py:106
  594.4 17.3 %collective-permute-start.4 = (f32[8,384,64]{1,2,0:T(8,128)}, f32[8,384,64]{1,2,0:T(8,128)}, u32[]{:S(2)}, u32[]{:S(2)}) collective-permute-start(f32[8,384,64]{1,2,0:T(8,128)} %get-tuple-element.1099), channel_id=1, source_target_pairs={{0,1},{1,2},{2,3},{3,4},{4,5},{5,6},{6,7},{7,0},{8,9},{9,10},{10,1... | collective-permute-start | bytes 2359304 | tf_op jit(solution)/shard_map/while/body/eval_jaxpr/ppermute | solution.py:106
  600.3 19.9 %collective-permute-start.5 = (bf16[384,8,64]{0,2,1:T(8,128)(2,1)S(1)}, bf16[384,8,64]{0,2,1:T(8,128)(2,1)}, u32[]{:S(2)}, u32[]{:S(2)}) collective-permute-start(bf16[384,8,64]{0,2,1:T(8,128)(2,1)S(1)} %copy.103), channel_id=1, source_target_pairs={{0,1},{1,2},{2,3},{3,4},{4,5},{5,6},{6,7},{7,0},{8,9},{9,10},{10,1... | collective-permute-start | bytes 1179656 | tf_op jit(solution)/shard_map/while/body/eval_jaxpr/ppermute | solution.py:106
  602.8 17.4 %collective-permute-start.6 = (bf16[384,8,64]{0,2,1:T(8,128)(2,1)}, bf16[384,8,64]{0,2,1:T(8,128)(2,1)}, u32[]{:S(2)}, u32[]{:S(2)}) collective-permute-start(bf16[384,8,64]{0,2,1:T(8,128)(2,1)} %copy.104), channel_id=1, source_target_pairs={{0,1},{1,2},{2,3},{3,4},{4,5},{5,6},{6,7},{7,0},{8,9},{9,10},{10,1... | collective-permute-start | bytes 1179656 | tf_op jit(solution)/shard_map/while/body/eval_jaxpr/ppermute | solution.py:106
  602.8 17.3 %collective-permute-start.7 = (s32[384]{0:T(512)S(1)}, s32[384]{0:T(512)S(1)}, u32[]{:S(2)}, u32[]{:S(2)}) collective-permute-start(s32[384]{0:T(512)S(1)} %copy.105), channel_id=1, source_target_pairs={{0,1},{1,2},{2,3},{3,4},{4,5},{5,6},{6,7},{7,0},{8,9},{9,10},{10,1... | collective-permute-start | bytes 4616 | tf_op jit(solution)/shard_map/while/body/eval_jaxpr/ppermute | solution.py:106
  623.4 7.2 collective-permute-start.9
  635.4 141.3 %reduce-scatter.7.cloned.1.call-start = ((), (), s32[]{:S(2)}) async-start(), calls=%async_computation.5 | async-start | bytes 4718592 | tf_op jit(solution)/shard_map/reduce_scatter | solution.py:128
  635.7 11.5 %collective-permute-start.8 = (f32[8,384,64]{1,2,0:T(8,128)S(1)}, f32[8,384,64]{1,2,0:T(8,128)S(1)}, u32[]{:S(2)}, u32[]{:S(2)}) collective-permute-start(f32[8,384,64]{1,2,0:T(8,128)S(1)} %get-tuple-element.836), channel_id=1, source_target_pairs={{0,1},{1,2},{2,3},{3,4},{4,5},{5,6},{6,7},{7,0},{8,9},{9,10},{10,1... | collective-permute-start | bytes 2359304 | tf_op jit(solution)/shard_map/ppermute | solution.py:114
  652.9 216.8 %reduce-scatter.5.cloned.1.call-start = ((), (), s32[]{:S(2)}) async-start(), calls=%async_computation.4 | async-start | bytes 18874368 | tf_op jit(solution)/shard_map/reduce_scatter | solution.py:128
  665.6 295.3 %reduce-scatter.11.cloned.1.call-start = ((), (), s32[]{:S(2)}) async-start(), calls=%async_computation.7 | async-start | bytes 18874368 | tf_op jit(solution)/shard_map/reduce_scatter | solution.py:128
  (10 other events, 44.6 us)
Sparse Core Ops, SparseCore 0:
  635.5 103.4 reduce-scatter.8
  741.9 34.8 reduce-scatter.6
  779.7 89.9 reduce-scatter.4
  872.5 88.3 reduce-scatter.10
where the time goes:
time: 980 us; the launch traced here: 968 us
  waiting for transfers between devices  402 us (41%)
  starting transfers between devices  214 us (22%)
  matrix products  192 us (20%)
  local copies, waits for them, and re-layouts  90.8 us (9%)
  other arithmetic  31.1 us (3%)
  loops' own time  20.1 us (2%)
  between operations  16.8 us (2%)
    reduce_scatter x4, waiting for transfers between devices, reduce_rows(): return lax.psum_scatter(part_sum, 'cp', scatter_dimension=0, tiled=True)  264 us
    ppermute x35, starting transfers between devices, backward_body(): lax.ppermute((k_blk, v_blk, seg_blk, dk_acc, dv_acc), 'cp', shift_pairs)  122 us
    ppermute x35, waiting for transfers between devices, backward_body(): lax.ppermute((k_blk, v_blk, seg_blk, dk_acc, dv_acc), 'cp', shift_pairs)  116 us
    ppermute x21, starting transfers between devices, forward_body(): lax.ppermute((k_blk, v_blk, seg_blk), 'cp', shift_pairs)  86.8 us
    another operation x44, local copies, waits for them, and re-layouts  38 us
    dot_general x2, matrix products, attend_block(): jnp.einsum('kqgs,skd->kqgd', weights.astype(jnp.bfloat16), v_blk, preferr...  27.6 us
    while x14, local copies, waits for them, and re-layouts  22.4 us
    dot_general x2, matrix products, attend_block(): jnp.einsum('qkgd,skd->kqgs', q_loc, k_blk, preferred_element_type=jnp.flo...  21.2 us
  transfers between devices with their start and end apart: 62, of which 31 were waited for; matrix products, arithmetic and copies ran while one was open for 17% of the time, Pallas kernels for 0%

commit v1 on v0

v1 whole, which is shorter than its diff:
```python
import functools

import jax
import jax.numpy as jnp
from jax import lax
from jax.experimental import pallas as pl
from jax.experimental.pallas import tpu as pltpu
from jax.sharding import PartitionSpec as P

BF = jnp.bfloat16
F32 = jnp.float32
LANES = 128
LOG2E = 1.4426950408889634
VMEM_MAX = 67043328


def rdma(src, dst, send_sem, recv_sem, peer):
    return pltpu.make_async_remote_copy(src_ref=src, dst_ref=dst, send_sem=send_sem, recv_sem=recv_sem,
                                        device_id={'cp': peer}, device_id_type=pl.DeviceIdType.MESH)


def dot_nt(left, right):
    return lax.dot_general(left, right, (((1,), (1,)), ((), ())), preferred_element_type=F32)


def dot_tn(left, right):
    return lax.dot_general(left, right, (((0,), (0,)), ((), ())), preferred_element_type=F32)


def dot_nn(left, right):
    return lax.dot_general(left, right, (((1,), (0,)), ((), ())), preferred_element_type=F32)


def pick(index, values):
    out = values[0]
    for k in range(1, len(values)):
        out = jnp.where(index == k, values[k], out)
    return out


def main_kernel(dims, x_ref, dy_ref, seg_ref, wq_ref, wk_ref, wv_ref, wo_ref,
                y_ref, dx_ref, dwq_ref, dwk_ref, dwv_ref, dwo_ref,
                seg_mine, seg_all, first_ref, kvn, pbuf, rhsq, rhsd, stats, oacc, dqacc, dkacc, dvacc,
                xall, qkv, gath, back, dyc, dyrel, dqrel, kvrel, frel, fpart, woa, wob,
                wsem, lsem, dyload, xsend, xrecv, xrelay, xpar, psend, precv, pfirst, psecond, gsend, grecv,
                ysend, yrecv, yfirst, ysecond, osem, relsem, parsem, rsem, dqsend, dqrecv, dqfirst, dqsecond,
                kvsend, kvrecv, kvfirst, kvsecond, fsend, frecv, ffirst, fsecond, outsem, free_far, free_par):
    n, qrows, krows, tok, scale = dims
    chips = n // 2
    heads = qrows // krows
    me = lax.axis_index('cp')
    chip, core = me // 2, me % 2
    sgn = 1 - 2 * core
    rows = 2 * qrows + 2 * krows
    width = rhsq.shape[2]
    group = width // tok
    pairs = heads // group
    prow = group * krows
    model = x_ref.shape[1]
    mcol = dyc.shape[1]
    half = tok // 2
    do0, kv0 = qrows, 2 * qrows
    remote = range(n - 1)

    def device(chip_off, flip):
        return ((chip + chip_off + chips) % chips) * 2 + (core + flip) % 2

    right, left, partner = device(1, 0), device(-1, 0), device(0, 1)
    dests = [device(2, 0), device(2, 1), device(-sgn, 0), device(-sgn, 1), device(sgn, 0), device(sgn, 1), partner]
    ahead = dests[4]
    relay_from = device(-sgn, 0)

    barrier = pltpu.get_barrier_semaphore()
    for peer in dests:
        pl.semaphore_signal(barrier, inc=1, device_id={'cp': peer}, device_id_type=pl.DeviceIdType.MESH)

    slot_table = (0, 4, 1, 2, 5, 6, 3, 7)
    off_table = (0, 0, chips - 1, 1, chips - 1, 1, 2, 2)
    flip_table = (0, 1, 0, 0, 1, 1, 0, 1)

    def source_of(order):
        return ((chip + pick(order, off_table)) % chips) * 2 + (core + pick(order, flip_table)) % 2

    def xhalf(ref, h):
        return ref.at[pl.ds(h * half, half)]

    def x_right(h):
        return rdma(xhalf(x_ref, h), xhalf(xall.at[me], h), xsend.at[0, h], xrecv.at[1, h], right)

    def x_left(h):
        return rdma(xhalf(x_ref, h), xhalf(xall.at[me], h), xsend.at[1, h], xrecv.at[2, h], left)

    def x_relay(h):
        tile, peer = (left, right) if h == 0 else (right, left)
        part = xhalf(xall.at[tile], h)
        return rdma(part, part, xrelay.at[h], xrecv.at[3, h], peer)

    def x_partner(slot):
        tile = (me, left, right, dests[0])[slot]
        src = x_ref if slot == 0 else xall.at[tile]
        return rdma(src, xall.at[tile], xpar.at[slot], xrecv.at[4 + slot, 0], partner)

    def do_tile(src):
        return qkv.at[src, pl.ds(do0, qrows)]

    def p_first(t):
        return rdma(gath.at[2, t], gath.at[6, t], psend.at[t], pfirst.at[t], ahead)

    def p_second(t):
        return rdma(gath.at[6, t], do_tile(relay_from), psecond.at[t], precv.at[relay_from], device(sgn, t))

    def p_direct(t):
        return rdma(gath.at[2, t], do_tile(me), psend.at[t], precv.at[me], dests[t])

    def do_arrived(src):
        rdma(gath.at[2, 0], do_tile(src), psend.at[0], precv.at[src], partner).wait_recv()

    def seg_copy(t):
        row = pl.ds(0, 1)
        return rdma(seg_mine.at[row], seg_all.at[me, row], gsend.at[t], grecv.at[t], dests[t])

    def columns(dst):
        return dy_ref.at[:, pl.ds(pl.multiple_of(dst * mcol, LANES), mcol)]

    def token_rows(src):
        return dyc.at[pl.ds(pl.multiple_of(src * tok, LANES), tok)]

    def y_first(t):
        return rdma(columns(dests[t]), dyrel.at[t], ysend.at[t], yfirst.at[t], ahead)

    def y_second(t):
        return rdma(dyrel.at[t], token_rows(relay_from), ysecond.at[t], yrecv.at[t], device(sgn, t))

    def y_direct(t):
        return rdma(columns(dests[t]), token_rows(me), ysend.at[t], yrecv.at[t], dests[t])

    def o_rows(pair, lo, size):
        return pl.ds(pl.multiple_of(pair * prow + lo, krows), size)

    def own_o(pair, j):
        return qkv.at[j, o_rows(pair, 0, prow)]

    def far_o(slot, pair, j, lo=0, size=None):
        return gath.at[slot - 1, j, o_rows(pair, lo, prow if size is None else size)]

    def own_right(pair, j):
        return rdma(own_o(pair, j), far_o(1, pair, j), osem.at[0, pair, j], rsem.at[1, pair, j], right)

    def own_left(pair, j):
        return rdma(own_o(pair, j), far_o(2, pair, j), osem.at[1, pair, j], rsem.at[2, pair, j], left)

    def relay_plus(pair, j):
        return rdma(far_o(1, pair, j, 0, krows), far_o(3, pair, j, 0, krows), relsem.at[0, pair, j], rsem.at[3, pair, j], right)

    def relay_minus(pair, j):
        return rdma(far_o(2, pair, j, krows, krows), far_o(3, pair, j, krows, krows), relsem.at[1, pair, j], rsem.at[0, pair, j], left)

    def to_partner(slot, pair, j):
        src = own_o(pair, j) if slot == 0 else far_o(slot, pair, j)
        return rdma(src, far_o(4 + slot, pair, j), parsem.at[slot, pair, j], rsem.at[4 + slot, pair, j], partner)

    def serve_near(pair, j):
        own_right(pair, j).wait_recv()
        relay_plus(pair, j).start()
        to_partner(1, pair, j).start()
        own_left(pair, j).wait_recv()
        relay_minus(pair, j).start()
        to_partner(2, pair, j).start()

    def serve_far(pair, j):
        relay_plus(pair, j).wait_recv()
        relay_minus(pair, j).wait_recv()
        to_partner(3, pair, j).start()

    def arrived(slot):
        for pair in range(pairs):
            for j in range(n):
                to_partner(slot - 4, pair, j).wait_recv()

    def dq_rows(pair):
        return pl.ds(pl.multiple_of(pair * prow, prow), prow)

    def dq_own(pair, j):
        return qkv.at[j, pl.ds(pl.multiple_of(do0 + pair * prow, prow), prow)]

    def dq_direct(pair, j):
        return rdma(dq_own(pair, j), back.at[me, dq_rows(pair)], dqsend.at[pair, j], dqrecv.at[pair, me], j)

    def dq_first(pair, j):
        return rdma(dq_own(pair, j), dqrel.at[pair, j % 2], dqsend.at[pair, j], dqfirst.at[pair, j % 2], ahead)

    def dq_second(pair, j):
        return rdma(dqrel.at[pair, j % 2], back.at[relay_from, dq_rows(pair)], dqsecond.at[pair, j % 2],
                    dqrecv.at[pair, relay_from], j)

    def send_dq(pair, j):
        owner_far = j // 2 == (chip + 2) % chips

        @pl.when(j == me)
        def _():
            back[me, dq_rows(pair)] = qkv[j, pl.ds(pl.multiple_of(do0 + pair * prow, prow), prow)]

        @pl.when(owner_far)
        def _():
            dq_first(pair, j).start()

        @pl.when((j != me) & jnp.logical_not(owner_far))
        def _():
            dq_direct(pair, j).start()

    def serve_dq(pair, j):
        @pl.when(j // 2 == (chip + sgn + chips) % chips)
        def _():
            dq_first(pair, j).wait_recv()
            dq_second(pair, j).start()

    def kv_own(src):
        return qkv.at[src, pl.ds(kv0, 2 * krows)]

    def kv_place(src):
        return back.at[src, pl.ds(qrows, 2 * krows)]

    def kv_first(t):
        return rdma(kv_own(dests[t]), kvrel.at[t], kvsend.at[t], kvfirst.at[t], ahead)

    def kv_second(t):
        return rdma(kvrel.at[t], kv_place(relay_from), kvsecond.at[t], kvrecv.at[t], device(sgn, t))

    def kv_direct(t):
        return rdma(kv_own(dests[t]), kv_place(me), kvsend.at[t], kvrecv.at[t], dests[t])

    def grad_places(part, owner):
        if part < pairs:
            return [(pl.ds(0, prow), dwq_ref.at[pl.ds(owner * qrows + part * prow, prow)], 0)]
        return [(pl.ds(0, krows), dwk_ref.at[pl.ds(owner * krows, krows)], 0),
                (pl.ds(krows, krows), dwv_ref.at[pl.ds(owner * krows, krows)], 1)]

    def block_ref(part, t):
        if part == 0:
            return fpart.at[t]
        return pbuf.at[1, 4 * (part - 1) + t // 3, pl.ds(0, prow), pl.ds(pl.multiple_of((t % 3) * mcol, LANES), mcol)]

    def f_first(part, t):
        return rdma(block_ref(part, t), frel.at[part, t], fsend.at[part, t, 0], ffirst.at[part, t], ahead)

    def f_second(part, t):
        return [rdma(frel.at[part, t, span], place, fsecond.at[part, t, k], frecv.at[part, t, k], device(sgn, t))
                for span, place, k in grad_places(part, relay_from)]

    def f_direct(part, t):
        return [rdma(block_ref(part, t).at[span], place, fsend.at[part, t, k], frecv.at[part, t, k], dests[t])
                for span, place, k in grad_places(part, me)]

    def f_own(part):
        return [pltpu.make_async_copy(block_ref(part, n - 1).at[span], place, outsem.at[part, k])
                for span, place, k in grad_places(part, me)]

    dest_off = (2, 2, -1, -1, 1, 1, 0, 0)
    dest_flip = (0, 1, 0, 1, 0, 1, 1, 0)

    def dest_of(t):
        return ((chip + sgn * pick(t, dest_off) + chips) % chips) * 2 + (core + pick(t, dest_flip)) % 2

    def weight_grads(part):
        lo = do0 + part * prow if part < pairs else kv0

        def block_step(t, carry):
            cols = pl.ds(pl.multiple_of(dest_of(t) * mcol, LANES), mcol)
            wide = jnp.concatenate([qkv[j, lo:lo + prow, :] for j in range(n)], axis=1)
            block_ref(part, t)[...] = dot_nn(wide, xall[:, :, cols].reshape(n * tok, mcol))
            for k in remote:
                @pl.when(t == k)
                def _():
                    for copy in [f_first(part, k)] if k < 2 else f_direct(part, k):
                        copy.start()

            @pl.when(t == n - 1)
            def _():
                for copy in f_own(part):
                    copy.start()
            return carry

        lax.fori_loop(0, n, block_step, 0)

    def relay_grads(part):
        for t in range(2):
            f_first(part, t).wait_recv()
            for copy in f_second(part, t):
                copy.start()

    def load(kind, order, buf):
        src = source_of(order)
        if kind == 0:
            return [pltpu.make_async_copy(wo_ref.at[pl.ds(src * qrows, qrows)], woa.at[buf], wsem.at[0, buf])]
        return [pltpu.make_async_copy(wq_ref.at[pl.ds(src * qrows, qrows)], wob.at[buf, pl.ds(0, qrows)], wsem.at[1, buf]),
                pltpu.make_async_copy(wk_ref.at[pl.ds(src * krows, krows)], wob.at[buf, pl.ds(qrows, krows)], wsem.at[2, buf]),
                pltpu.make_async_copy(wv_ref.at[pl.ds(src * krows, krows)], wob.at[buf, pl.ds(qrows + krows, krows)], wsem.at[3, buf])]

    parts = [(j, slice(j * width, min((j + 1) * width, model))) for j in range(-(-model // width))]

    def stage(buf):
        return pbuf.at[0, 6, pl.ds(0, qrows), pl.ds(pl.multiple_of(buf * mcol, LANES), mcol)]

    def save(order, buf):
        return pltpu.make_async_copy(stage(buf), dwo_ref.at[pl.ds(source_of(order) * qrows, qrows)], wsem.at[4, buf])

    def next_weights(kind, order):
        buf = order % 2
        for copy in load(kind, order, buf):
            copy.wait()

        @pl.when(order < n - 1)
        def _():
            for copy in load(kind, order + 1, 1 - buf):
                copy.start()

        return buf

    def close_o(order, own):
        buf = next_weights(0, order)
        slot = pick(order, slot_table)

        def tile_o(j):
            return qkv[j, 0:qrows, :] if own else gath[slot - 1, j]

        @pl.when(order >= 2)
        def _():
            save(order - 2, buf).wait()

        @pl.when(order >= 0)
        def _():
            stage(buf)[...] = dot_nn(jnp.concatenate([tile_o(j) for j in range(n)], axis=1), dyc[...])

        save(order, buf).start()
        for j, cols in parts:
            @pl.when(order >= 0)
            def _():
                pbuf[0, j, :, 0:cols.stop - cols.start] += dot_tn(tile_o(me), woa[buf, :, cols])

    def close_dx(order):
        buf = next_weights(1, order)
        for j, cols in parts:
            @pl.when(order >= 0)
            def _():
                pbuf[0, 3 + j, :, 0:cols.stop - cols.start] += dot_tn(back[source_of(order)], wob[buf, :, cols])

    def do_weights(t, buf):
        return pltpu.make_async_copy(wo_ref.at[pl.ds(dest_of(t) * qrows, qrows)], woa.at[buf], wsem.at[0, buf])

    dy_cols = [(c, c * tok, min(tok, model - c * tok)) for c in range(-(-model // tok))]
    dy_in = [pltpu.make_async_copy(dy_ref.at[:, pl.ds(lo, size)], back.at[c, :, pl.ds(0, size)], dyload.at[c])
             for c, lo, size in dy_cols]
    x_in = pltpu.make_async_copy(x_ref, xall.at[me], lsem.at[1])
    y_own = pltpu.make_async_copy(columns(me), token_rows(me), lsem.at[2])
    own_weights = [pltpu.make_async_copy(wq_ref.at[pl.ds(me * qrows, qrows)], wob.at[0, pl.ds(0, qrows)], lsem.at[3]),
                   pltpu.make_async_copy(wk_ref.at[pl.ds(me * krows, krows)], wob.at[0, pl.ds(qrows, krows)], lsem.at[4]),
                   pltpu.make_async_copy(wv_ref.at[pl.ds(me * krows, krows)], wob.at[0, pl.ds(qrows + krows, krows)], lsem.at[5])]
    for copy in dy_in:
        copy.start()
    do_weights(0, 0).start()
    for copy in [x_in, y_own] + own_weights:
        copy.start()
    seg_mine[...] = jnp.broadcast_to(seg_ref[...].reshape(1, tok), seg_mine.shape)
    pl.semaphore_wait(barrier, n - 1)
    for h in range(2):
        x_right(h).start()
        x_left(1 - h).start()
    x_partner(0).start()
    for t in remote:
        seg_copy(t).start()
    seg_all[me] = seg_mine[...]
    for copy in dy_in:
        copy.wait()

    def do_step(t, carry):
        buf = t % 2

        @pl.when(t < n - 1)
        def _():
            do_weights(t + 1, 1 - buf).start()

        do_weights(t, buf).wait()
        local = jnp.concatenate([back[c, :, 0:size] for c, lo, size in dy_cols], axis=1)
        block = dot_nt(woa[buf], local).astype(BF)

        @pl.when(t < n - 1)
        def _():
            gath[2, t] = block

        @pl.when(t == n - 1)
        def _():
            qkv[me, do0:kv0] = block
        return carry

    lax.fori_loop(0, n, do_step, 0)
    dkacc[...] = jnp.zeros_like(dkacc)
    dvacc[...] = jnp.zeros_like(dvacc)
    rhsq[...] = jnp.zeros_like(rhsq)
    rhsd[...] = jnp.zeros_like(rhsd)
    for copy in [x_in] + own_weights:
        copy.wait()

    def project_step(order, carry):
        @pl.when(order == 1)
        def _():
            x_partner(0).wait_recv()

        @pl.when(order == 2)
        def _():
            x_right(0).wait_recv()
            x_relay(0).start()
            x_left(1).wait_recv()
            x_relay(1).start()
            for t in remote:
                (p_first if t < 2 else p_direct)(t).start()
            x_right(1).wait_recv()
            x_partner(1).start()

        @pl.when(order == 3)
        def _():
            x_left(0).wait_recv()
            x_partner(2).start()

        @pl.when(order == 4)
        def _():
            x_partner(1).wait_recv()

        @pl.when(order == 5)
        def _():
            x_partner(2).wait_recv()

        @pl.when(order == 6)
        def _():
            for h in range(2):
                x_relay(h).wait_recv()
            x_partner(3).start()
            for t in range(2):
                p_first(t).wait_recv()
                p_second(t).start()

        @pl.when(order == 7)
        def _():
            x_partner(3).wait_recv()

        src = source_of(order)
        qkv[src, 0:qrows] = dot_nt(wob[0, 0:qrows], xall[src]).astype(BF)
        kv = dot_nt(wob[0, qrows:qrows + 2 * krows], xall[src]).astype(BF)
        qkv[src, kv0:rows] = kv
        kvn[pl.ds(pl.multiple_of(src * tok, LANES), tok), :] = kv.T
        return carry

    lax.fori_loop(0, n, project_step, 0)
    for t in remote:
        (y_first if t < 2 else y_direct)(t).start()

    for t in remote:
        seg_copy(t).wait_recv()
    row_id = lax.broadcasted_iota(jnp.int32, (n, tok), 0)
    lane_id = lax.broadcasted_iota(jnp.int32, (n, tok), 1)
    seg = jnp.zeros((n, tok), jnp.int32)
    for d in range(n):
        seg = jnp.where(row_id == d, seg_all[d, 0:1], seg)
    before = jnp.where(lane_id == 0, pltpu.roll(pltpu.roll(seg, 1, 1), 1, 0), pltpu.roll(seg, 1, 1))
    pos = row_id * tok + lane_id
    best = jnp.where((seg != before) & (pos > 0), pos, 0)
    shift = 1
    while shift < tok:
        best = jnp.maximum(best, jnp.where(lane_id >= shift, pltpu.roll(best, shift, 1), 0))
        shift *= 2
    end = jnp.broadcast_to(best[:, tok - 1:tok], (n, tok))
    carry_max = jnp.where(row_id >= 1, pltpu.roll(end, 1, 0), 0)
    shift = 1
    while shift < n:
        carry_max = jnp.maximum(carry_max, jnp.where(row_id >= shift, pltpu.roll(carry_max, shift, 0), 0))
        shift *= 2
    best = jnp.maximum(best, carry_max)
    for d in range(n):
        first_ref[d] = jnp.broadcast_to(best[d:d + 1], (8, tok))

    score_mul = scale * LOG2E
    grp = tok // 8
    lag = 2

    def keys(c):
        return kvn[pl.ds(pl.multiple_of(c * tok, LANES), tok), :]

    def q_rows(pair, g):
        return pl.ds(pl.multiple_of((pair * group + g) * krows, krows), krows)

    def do_rows(pair, g):
        return pl.ds(pl.multiple_of(do0 + (pair * group + g) * krows, krows), krows)

    def doc_starts(i):
        return jnp.concatenate([first_ref[i][0:1]] * group, axis=1)

    def score(i, par, c, top, diagonal):
        t = dot_nn(keys(c), rhsq[par]) * score_mul
        kpos = lax.broadcasted_iota(jnp.int32, (tok, width), 0)
        keep = kpos >= doc_starts(i) - c * tok
        if diagonal:
            qpos = lax.broadcasted_iota(jnp.int32, (1, tok), 1)
            keep = keep & (kpos <= jnp.concatenate([qpos] * group, axis=1))
        t = jnp.where(keep, t, -jnp.inf)
        pbuf[par, c] = t
        return jnp.maximum(top, jnp.max(t.reshape(grp, 8, width), axis=0))

    def value(par, c, top, total):
        p = jnp.exp2(pbuf[par, c] - top)
        oacc[...] += dot_nn(qkv[c, kv0 + krows:rows, :], p.astype(BF))
        return total + jnp.sum(p.reshape(grp, 8, width), axis=0)

    def grad(par, c):
        p = jnp.exp2(pbuf[par, c] - stats[par, 0:1])
        dp = dot_nn(keys(c), rhsd[par])
        ds = (p * (dp - stats[par, 8:9])).astype(BF)
        dqacc[...] += dot_nn(qkv[c, kv0:kv0 + krows, :], ds)
        pb = p.astype(BF)
        spans = [(slice(j * mcol, (j + 1) * mcol), slice(j * tok, (j + 1) * tok)) for j in range(width // mcol)]
        for qs, place in spans:
            woa[0, :, place] = ds[:, qs].T
            wob[0, 0:mcol, place] = pb[:, qs].T
        dkacc[c] += sum(dot_nn(rhsq[par, 0:krows, qs], woa[0, :, place]) for qs, place in spans)
        dvacc[c] += sum(dot_nn(rhsd[par, krows:2 * krows, qs], wob[0, 0:mcol, place]) for qs, place in spans)

    def tile_done(pair, j):
        dq = (dqacc[...] * scale).astype(BF)
        for g in range(group):
            qkv[j, do_rows(pair, g), :] = dq[:, g * tok:(g + 1) * tok]
        piece = pair * n + j

        @pl.when(piece == 0)
        def _():
            for t in remote:
                p_direct(t).wait_send()
            for t in range(2):
                p_second(t).wait_send()
            for peer in (right, left):
                pl.semaphore_signal(free_far, inc=1, device_id={'cp': peer}, device_id_type=pl.DeviceIdType.MESH)
            pl.semaphore_signal(free_par, inc=1, device_id={'cp': partner}, device_id_type=pl.DeviceIdType.MESH)

        own_right(pair, j).start()
        own_left(pair, j).start()
        to_partner(0, pair, j).start()
        send_dq(pair, j)

        @pl.when(piece == 1)
        def _():
            for t in range(2):
                y_first(t).wait_recv()
                y_second(t).start()

        @pl.when(piece == lag)
        def _():
            pl.semaphore_wait(free_far, 2)

        @pl.when(piece == n + 1)
        def _():
            relay_grads(0)

        @pl.when(piece >= lag)
        def _():
            old = piece - lag
            serve_near(old // n, old % n)
            serve_dq(old // n, old % n)

    def item_step(m, carry):
        pair, i = m // n, m % n
        par = i % 2
        last = 1 - par

        @pl.when((pair == 0) & (i != me))
        def _():
            do_arrived(i)

        for g in range(group):
            lanes = slice(g * tok, (g + 1) * tok)
            rhsq[par, 0:krows, lanes] = qkv[i, q_rows(pair, g), :]
            rhsd[par, krows:2 * krows, lanes] = qkv[i, do_rows(pair, g), :]
        dqacc[...] = jnp.zeros_like(dqacc)

        def both_step(c, top):
            grad(last, c)
            return score(i, par, c, top, False)

        top = lax.fori_loop(0, i, both_step, jnp.full((8, width), -jnp.inf, F32))
        top = score(i, par, i, top, True)

        @pl.when(i >= 1)
        def _():
            tile_done(pair, i - 1)

        top = jnp.max(top, axis=0, keepdims=True)
        oacc[...] = jnp.zeros_like(oacc)
        total = lax.fori_loop(0, i + 1, lambda c, acc: value(par, c, top, acc), jnp.zeros((8, width), F32))
        total = jnp.sum(total, axis=0, keepdims=True)
        o_blk = (oacc[...] * (1.0 / total)).astype(BF)
        stats[par, 0:8] = jnp.broadcast_to(top + jnp.log2(total), (8, width))
        delta = jnp.sum(rhsd[par, krows:2 * krows].astype(F32) * o_blk.astype(F32), axis=0, keepdims=True)
        stats[par, 8:16] = jnp.broadcast_to(delta, (8, width))
        for g in range(group):
            qkv[i, q_rows(pair, g), :] = o_blk[:, g * tok:(g + 1) * tok]

        @pl.when(i == n - 1)
        def _():
            dqacc[...] = jnp.zeros_like(dqacc)

            def last_step(c, inner):
                grad(par, c)
                return inner

            lax.fori_loop(0, n, last_step, 0)
            tile_done(pair, i)

        @pl.when(m == n - 1)
        def _():
            weight_grads(0)
        return carry

    lax.fori_loop(0, n * pairs, item_step, 0)

    for c in range(n):
        qkv[c, kv0:kv0 + krows, :] = (dkacc[c] * scale).astype(BF)
        qkv[c, kv0 + krows:rows, :] = dvacc[c].astype(BF)
    for t in remote:
        (kv_first if t < 2 else kv_direct)(t).start()
    back[me, qrows:qrows + 2 * krows] = qkv[me, kv0:rows]
    for kind in range(2):
        for copy in load(kind, 0, 0):
            copy.start()
    for part in range(1, pairs + 1):
        weight_grads(part)
    for old in range(n * pairs - lag, n * pairs):
        serve_near(old // n, old % n)
        serve_dq(old // n, old % n)
    for t in range(2):
        kv_first(t).wait_recv()
        kv_second(t).start()
    pbuf[0, 0:6] = jnp.zeros((6, tok, width), F32)
    y_own.wait()
    for t in remote:
        y_direct(t).wait_recv()

    def closing_step(r, carry):
        @pl.when(r == 1)
        def _():
            arrived(4)
            relay_grads(1)

        @pl.when(r == 2)
        def _():
            relay_grads(2)

        @pl.when(r == 4)
        def _():
            pl.semaphore_wait(free_par, 1)
            for pair in range(pairs):
                for j in range(n):
                    serve_far(pair, j)
            arrived(5)

        @pl.when(r == 5)
        def _():
            arrived(6)

        @pl.when(r == 7)
        def _():
            arrived(7)

        @pl.when(r == 0)
        def _():
            close_o(r, True)

        @pl.when((r >= 1) & (r < n))
        def _():
            close_o(r, False)

        @pl.when(r == n)
        def _():
            for t in remote:
                for pair in range(pairs):
                    rdma(dqrel.at[pair, 0], back.at[dests[t], dq_rows(pair)], dqsend.at[pair, 0],
                         dqrecv.at[pair, dests[t]], partner).wait_recv()
                kv_direct(t).wait_recv()

        @pl.when(r >= n)
        def _():
            close_dx(r - n)
        return carry

    lax.fori_loop(0, 2 * n, closing_step, 0)

    spare = tok - qrows

    def rounded(acc, buf, out, sem):
        for j, cols in parts:
            wide = pbuf[0, acc + j, :, 0:cols.stop - cols.start].astype(BF)
            buf[0, 0:qrows, cols] = wide[0:qrows]
            buf[1, 0:spare, cols] = wide[qrows:tok]
        return [pltpu.make_async_copy(buf.at[0, pl.ds(0, qrows)], out.at[pl.ds(0, qrows)], lsem.at[sem]),
                pltpu.make_async_copy(buf.at[1, pl.ds(0, spare)], out.at[pl.ds(qrows, spare)], lsem.at[sem + 1])]

    outs = rounded(0, woa, y_ref, 0) + rounded(3, wob, dx_ref, 2)
    for copy in outs:
        copy.start()

    for t in remote:
        seg_copy(t).wait_send()
        y_direct(t).wait_send()
        kv_direct(t).wait_send()
        for pair in range(pairs):
            rdma(dq_own(pair, 0), dqrel.at[pair, 0], dqsend.at[pair, dests[t]], dqfirst.at[pair, 0], partner).wait_send()
    for h in range(2):
        x_right(h).wait_send()
        x_left(h).wait_send()
        x_relay(h).wait_send()
    for slot in range(4):
        x_partner(slot).wait_send()
    for t in range(2):
        y_second(t).wait_send()
        kv_second(t).wait_send()
        for pair in range(pairs):
            dq_second(pair, t).wait_send()
    for pair in range(pairs):
        for j in range(n):
            own_right(pair, j).wait_send()
            own_left(pair, j).wait_send()
            relay_plus(pair, j).wait_send()
            relay_minus(pair, j).wait_send()
            for slot in range(4):
                to_partner(slot, pair, j).wait_send()
    for order in (n - 2, n - 1):
        save(order, order % 2).wait()
    for copy in outs:
        copy.wait()
    for part in range(pairs + 1):
        for copy in f_own(part):
            copy.wait()
        for t in remote:
            for copy in f_direct(part, t):
                copy.wait_recv()
        for t in range(2, n - 1):
            for copy in f_direct(part, t):
                copy.wait_send()
        for t in range(2):
            f_first(part, t).wait_send()
            for copy in f_second(part, t):
                copy.wait_send()


def attention_layer(n, x_act, dy_act, seg, wq, wk, wv, wo):
    tok, model = x_act.shape
    qrows, krows = wq.shape[0] // n, wk.shape[0] // n
    rows = 2 * qrows + 2 * krows
    total = n * tok
    mcol = model // n
    group = 2
    width = group * tok
    pairs = qrows // krows // group
    prow = group * krows
    vmem = pl.BlockSpec(memory_space=pltpu.VMEM)
    anym = pl.BlockSpec(memory_space=pl.ANY)
    dma = pltpu.SemaphoreType.DMA
    return pl.pallas_call(
        functools.partial(main_kernel, (n, qrows, krows, tok, krows ** -0.5)),
        out_shape=(jax.ShapeDtypeStruct((tok, model), BF), jax.ShapeDtypeStruct((tok, model), BF),
                   jax.ShapeDtypeStruct((wq.shape[0], mcol), F32), jax.ShapeDtypeStruct((wk.shape[0], mcol), F32),
                   jax.ShapeDtypeStruct((wv.shape[0], mcol), F32), jax.ShapeDtypeStruct((wo.shape[0], mcol), F32)),
        in_specs=[anym, anym, vmem, anym, anym, anym, anym],
        out_specs=(anym,) * 6,
        scratch_shapes=[
            pltpu.VMEM((8, tok), jnp.int32), pltpu.VMEM((n, 8, tok), jnp.int32), pltpu.VMEM((n, 8, tok), jnp.int32),
            pltpu.VMEM((total, 2 * krows), BF),
            pltpu.VMEM((2, n, tok, width), F32),
            pltpu.VMEM((2, 2 * krows, width), BF), pltpu.VMEM((2, 2 * krows, width), BF),
            pltpu.VMEM((2, 16, width), F32),
            pltpu.VMEM((krows, width), F32), pltpu.VMEM((krows, width), F32),
            pltpu.VMEM((n, krows, tok), F32), pltpu.VMEM((n, krows, tok), F32),
            pltpu.VMEM((n, tok, model), BF),
            pltpu.VMEM((n, rows, tok), BF),
            pltpu.VMEM((n - 1, n, qrows, tok), BF),
            pltpu.VMEM((n, qrows + 2 * krows, tok), BF),
            pltpu.VMEM((total, mcol), BF),
            pltpu.VMEM((2, tok, mcol), BF),
            pltpu.VMEM((pairs, 2, prow, tok), BF),
            pltpu.VMEM((2, 2 * krows, tok), BF),
            pltpu.VMEM((pairs + 1, 2, prow, mcol), F32),
            pltpu.VMEM((n, prow, mcol), F32),
            pltpu.VMEM((2, qrows, model), BF), pltpu.VMEM((2, qrows + 2 * krows, model), BF),
            dma((5, 2)), dma((6,)), dma((n,)),
            dma((2, 2)), dma((8, 2)), dma((2,)), dma((4,)),
            dma((n,)), dma((n,)), dma((2,)), dma((2,)), dma((n,)), dma((n,)),
            dma((n,)), dma((n,)), dma((2,)), dma((2,)),
            dma((2, pairs, n)), dma((2, pairs, n)), dma((4, pairs, n)), dma((8, pairs, n)),
            dma((pairs, n)), dma((pairs, n)), dma((pairs, 2)), dma((pairs, 2)),
            dma((n,)), dma((n,)), dma((2,)), dma((2,)),
            dma((pairs + 1, n, 2)), dma((pairs + 1, n, 2)), dma((pairs + 1, 2)), dma((pairs + 1, 2, 2)), dma((pairs + 1, 2)),
            pltpu.SemaphoreType.REGULAR, pltpu.SemaphoreType.REGULAR,
        ],
        compiler_params=pltpu.CompilerParams(collective_id=0, has_side_effects=True, vmem_limit_bytes=VMEM_MAX),
        name='attention_layer',
    )(x_act, dy_act, seg, wq, wk, wv, wo)


def copy_out(arrays):
    pieces = 4
    count = len(arrays)

    def kernel(*refs):
        src, dst, buf = refs[:count], refs[count:2 * count], refs[2 * count:3 * count]
        insem, outsem = refs[3 * count:]
        loads, stores = [], []
        for k, array in enumerate(arrays):
            size = array.shape[0] // pieces
            for p in range(pieces):
                rows = pl.ds(p * size, size)
                loads.append(pltpu.make_async_copy(src[k].at[rows], buf[k].at[rows], insem.at[k, p]))
                stores.append(pltpu.make_async_copy(buf[k].at[rows], dst[k].at[rows], outsem.at[k, p]))
        for copy in loads:
            copy.start()
        for copy, store in zip(loads, stores):
            copy.wait()
            store.start()
        for store in stores:
            store.wait()

    anym = pl.BlockSpec(memory_space=pl.ANY)
    return pl.pallas_call(
        kernel,
        out_shape=tuple(jax.ShapeDtypeStruct(a.shape, a.dtype) for a in arrays),
        in_specs=[anym] * count, out_specs=(anym,) * count,
        scratch_shapes=[pltpu.VMEM(a.shape, a.dtype) for a in arrays]
        + [pltpu.SemaphoreType.DMA((count, pieces)), pltpu.SemaphoreType.DMA((count, pieces))],
        compiler_params=pltpu.CompilerParams(vmem_limit_bytes=VMEM_MAX),
        name='copy_out',
    )(*arrays)


def solution(mesh):
    n = mesh.shape['cp']
    row_spec = P(('dp', 'cp'), None)
    tok_spec = P(('dp', 'cp'))
    weight_spec = P(None, None, None)
    grad_spec = P(('dp', 'cp'), None, None)

    def local_step(x_act, seg_ids, w_q, w_k, w_v, w_o, dy_act):
        model, q_heads, head_dim = w_q.shape
        kv_heads = w_k.shape[1]
        assert kv_heads == n and x_act.shape[0] % LANES == 0

        def flat(w):
            return w.transpose(1, 2, 0).reshape(w.shape[1] * head_dim, model)

        def unflat(g, heads):
            return g.reshape(heads, head_dim, g.shape[1]).transpose(2, 0, 1)

        wq, wk, wv, wo = flat(w_q), flat(w_k), flat(w_v), flat(w_o)
        y_out, dx_out, dwq, dwk, dwv, dwo = copy_out(attention_layer(n, x_act, dy_act, seg_ids, wq, wk, wv, wo))
        return (y_out, dx_out, unflat(dwq, q_heads), unflat(dwk, kv_heads), unflat(dwv, kv_heads), unflat(dwo, q_heads))

    return jax.shard_map(local_step, mesh=mesh,
                         in_specs=(row_spec, tok_spec, weight_spec, weight_spec, weight_spec, weight_spec, row_spec),
                         out_specs=(row_spec, row_spec, grad_spec, grad_spec, grad_spec, grad_spec),
                         check_vma=False)
```

time: 980 us -> 253 us (0.26); the launches traced: 968 us -> 252 us
  waiting for transfers between devices: 402 us -> 0 us
  Pallas kernels: 0 us -> 251 us
  starting transfers between devices: 214 us -> 0 us
  matrix products: 192 us -> 0 us
  local copies, waits for them, and re-layouts: 90.8 us -> 0 us
  other arithmetic: 31.1 us -> 0 us
  loops' own time: 20.1 us -> 0 us
  between operations: 16.8 us -> 0.8 us
    reduce_scatter x4 -> x0, waiting for transfers between devices: 264 us -> none  [reduce_rows(): return lax.psum_scatter(part_sum, 'cp', scatter_dimension=0, tiled=True)]
    pallas_call x0 -> x2, Pallas kernels: none -> 251 us  [the longest x1 244 us: attention_layer(): pl.pallas_call(functools.partial(main_kernel, (n, qrows, krows, tok, krow...]
    ppermute x58 -> x0, starting transfers between devices: 214 us -> none  [the longest x35 122 us: backward_body(): lax.ppermute((k_blk, v_blk, seg_blk, dk_acc, dv_acc), 'cp', shift_pairs)]
    dot_general x22 -> x0, matrix products: 173 us -> none  [the longest x2 27.6 us: attend_block(): jnp.einsum('kqgs,skd->kqgd', weights.astype(jnp.bfloat16), v_blk, preferr...]
    ppermute x58 -> x0, waiting for transfers between devices: 138 us -> none  [the longest x35 116 us: backward_body(): lax.ppermute((k_blk, v_blk, seg_blk, dk_acc, dv_acc), 'cp', shift_pairs)]
    another operation x44 -> x0, local copies, waits for them, and re-layouts: 38 us -> none
    slice x31 -> x0, local copies, waits for them, and re-layouts: 23.4 us -> none  [the longest x16 14.3 us: block_active(): seg_k[-1] == seg_q[0]]
    while x14 -> x0, local copies, waits for them, and re-layouts: 22.4 us -> none
  transfers between devices with their start and end apart: 62 -> 0, of which waited for: 31 -> 0; matrix products, arithmetic and copies ran while one was open for 17% -> 0% of each run, Pallas kernels for 0% -> 0%
where the time goes in v1:
time: 253 us; the launch traced here: 252 us
  Pallas kernels  251 us (99%)
    pallas_call x1, Pallas kernels, attention_layer(): pl.pallas_call(functools.partial(main_kernel, (n, qrows, krows, tok, krow...  244 us
    pallas_call x1, Pallas kernels, copy_out(): pl.pallas_call(kernel, out_shape=tuple((jax.ShapeDtypeStruct(a.shape, a.d...  6.92 us

profile of v1, /device:TPU:81, one launch (start us, length us, event | category | flops | bytes accessed | tf_op | source)
XLA Modules:
  0.0 251.5 jit_solution(14984762362131493484)
XLA Ops:
  0.6 243.8 %attention_layer.1 = (bf16[384,2048]{1,0:T(8,128)(2,1)}, bf16[384,2048]{1,0:T(8,128)(2,1)}, f32[2048,256]{1,0:T(8,128)}, f32[512,256]{1,0:T(8,128)}, f32[512,256]{1,0:T(8,128)}, /*index=5*/f32[2048,256]{1,0:T(8,128)}) custom-call(bf16[384,2048]{1,0:T(8,128)(2,1)} %x_ref.1, bf16[384,2048]{1,0:T(8,128)(2,1)} %dy_ref.1, s32[384]{0:T(512)} %seg_ref.1, ...), custom_call_target="tpu_custom_call" | custom-call | tf_op jit(solution)/shard_map/attention_layer/pallas_call | solution.py:763
  244.4 6.9 %copy_out.1 = (bf16[384,2048]{1,0:T(8,128)(2,1)}, bf16[384,2048]{1,0:T(8,128)(2,1)}, f32[2048,256]{1,0:T(8,128)}, f32[512,256]{1,0:T(8,128)}, f32[512,256]{1,0:T(8,128)}, /*index=5*/f32[2048,256]{1,0:T(8,128)}) custom-call(bf16[384,2048]{1,0:T(8,128)(2,1)} %get-tuple-element.18.refs_0_, bf16[384,2048]{1,0:T(8,128)(2,1)} %get-tuple-element.19.refs_1_, ...), custom_call_target="tpu_custom_call" | custom-call | tf_op jit(solution)/shard_map/copy_out/pallas_call | solution.py:827

commit v2 on v1

--- a/solution.py
+++ b/solution.py
@@ -393,6 +393,8 @@
         return carry
 
     lax.fori_loop(0, n, do_step, 0)
+    for t in remote:
+        (p_first if t < 2 else p_direct)(t).start()
     dkacc[...] = jnp.zeros_like(dkacc)
     dvacc[...] = jnp.zeros_like(dvacc)
     rhsq[...] = jnp.zeros_like(rhsq)
@@ -411,8 +413,6 @@
             x_relay(0).start()
             x_left(1).wait_recv()
             x_relay(1).start()
-            for t in remote:
-                (p_first if t < 2 else p_direct)(t).start()
             x_right(1).wait_recv()
             x_partner(1).start()
 
@@ -427,6 +427,9 @@
 
         @pl.when(order == 5)
         def _():
+            for t in range(2):
+                p_first(t).wait_recv()
+                p_second(t).start()
             x_partner(2).wait_recv()
 
         @pl.when(order == 6)
@@ -434,9 +437,6 @@
             for h in range(2):
                 x_relay(h).wait_recv()
             x_partner(3).start()
-            for t in range(2):
-                p_first(t).wait_recv()
-                p_second(t).start()
 
         @pl.when(order == 7)
         def _():
@@ -479,7 +479,7 @@
 
     score_mul = scale * LOG2E
     grp = tok // 8
-    lag = 2
+    lag = 5
 
     def keys(c):
         return kvn[pl.ds(pl.multiple_of(c * tok, LANES), tok), :]
@@ -543,7 +543,7 @@
         to_partner(0, pair, j).start()
         send_dq(pair, j)
 
-        @pl.when(piece == 1)
+        @pl.when(piece == lag)
         def _():
             for t in range(2):
                 y_first(t).wait_recv()
@@ -553,7 +553,7 @@
         def _():
             pl.semaphore_wait(free_far, 2)
 
-        @pl.when(piece == n + 1)
+        @pl.when(piece == n + lag + 1)
         def _():
             relay_grads(0)
 

time: 253 us -> 245 us (0.968)
  Pallas kernels: 251 us -> 243 us
    pallas_call x1, Pallas kernels: 244 us -> 236 us  [attention_layer(): pl.pallas_call(functools.partial(main_kernel, (n, qrows, krows, tok, krow...]
where the time goes in v2:
time: 245 us; the launch traced here: 244 us
  Pallas kernels  243 us (99%)
    pallas_call x1, Pallas kernels, attention_layer(): pl.pallas_call(functools.partial(main_kernel, (n, qrows, krows, tok, krow...  236 us
    pallas_call x1, Pallas kernels, copy_out(): pl.pallas_call(kernel, out_shape=tuple((jax.ShapeDtypeStruct(a.shape, a.d...  6.92 us

profile of v2, /device:TPU:81, one launch (start us, length us, event | category | flops | bytes accessed | tf_op | source)
XLA Modules:
  0.0 244.1 jit_solution(5646697373252226050)
XLA Ops:
  0.6 236.4 %attention_layer.1 = (bf16[384,2048]{1,0:T(8,128)(2,1)}, bf16[384,2048]{1,0:T(8,128)(2,1)}, f32[2048,256]{1,0:T(8,128)}, f32[512,256]{1,0:T(8,128)}, f32[512,256]{1,0:T(8,128)}, /*index=5*/f32[2048,256]{1,0:T(8,128)}) custom-call(bf16[384,2048]{1,0:T(8,128)(2,1)} %x_ref.1, bf16[384,2048]{1,0:T(8,128)(2,1)} %dy_ref.1, s32[384]{0:T(512)} %seg_ref.1, ...), custom_call_target="tpu_custom_call" | custom-call | tf_op jit(solution)/shard_map/attention_layer/pallas_call | solution.py:763
  237.0 6.9 %copy_out.1 = (bf16[384,2048]{1,0:T(8,128)(2,1)}, bf16[384,2048]{1,0:T(8,128)(2,1)}, f32[2048,256]{1,0:T(8,128)}, f32[512,256]{1,0:T(8,128)}, f32[512,256]{1,0:T(8,128)}, /*index=5*/f32[2048,256]{1,0:T(8,128)}) custom-call(bf16[384,2048]{1,0:T(8,128)(2,1)} %get-tuple-element.18.refs_0_, bf16[384,2048]{1,0:T(8,128)(2,1)} %get-tuple-element.19.refs_1_, ...), custom_call_target="tpu_custom_call" | custom-call | tf_op jit(solution)/shard_map/copy_out/pallas_call | solution.py:827
